TPU v7x, 256 devices: a whole 4x4x8 slice. The times are simulated.
256 devices in a mesh: task: 8 (over y, core), col: 32 (over z, x).
Axes of the slice: x: 4, y: 4, z: 8, core: 2. Of those that a mesh axis runs over, the one named last changes fastest.
Arguments:
- layer_inputs: bfloat16 [8, 1024, 8192], P('task', None, 'col'), may hold values from -6 to 6
- queries: bfloat16 [8, 1024, 8192], P('task', None, 'col'), may hold values from -1000 to 1000, as said below
- key_values: bfloat16 [8, 1024, 2048], P('task', 'col'), may hold values from -8 to 8, as said below
- out_grads: bfloat16 [8, 1024, 8192], P('task', None, 'col'), may hold values from -0.29882812 to 0.29882812
- lengths: int32 [8, 4], P('task'), may hold values from 1 to 512, 1024 in all within a row
- task_weights: bfloat16 [8, 8192, 2048], P('task', 'col'), may hold values from -6 to 6
Outputs:
- fisher: float32 [8, 8192, 2048], P('task', 'col')
- merged: bfloat16 [8192, 2048], P('col')
Inputs may be any that keep to these rules, and one draw needn't show every extreme that they name: `queries`: queries of every head for the tokens of each task. `key_values`: keys and values of every head for the tokens of each task.
All inputs are finite; a program needn't handle non-finite values.
Results may differ from a plain program's by a relative error of at most 0.02.
Values may be sent and summed in bfloat16 or wider, within the bound.
A program may use at most 64 MiB of HBM per device.

v0:
```python
import jax
import jax.numpy as jnp
from jax import lax
from jax.sharding import Mesh
from jax.sharding import PartitionSpec as P

KVH = 8
HD = 128
COL = ("col_0", "col_1")


EPS = 1e-06
NEGATIVE = -1e30


def gather_axes(array, axes, dim):
    if not axes:
        return array
    nearer = lax.all_gather(array, axes[-1], axis=dim, tiled=True)
    return gather_axes(nearer, axes[:-1], dim)


def split_up(array, dim, count):
    dims = array.shape
    tiles = array.reshape(*dims[:dim], count, dims[dim] // count, *dims[dim + 1 :])
    return jnp.moveaxis(tiles, dim, 0)


def sent_and_summed(array, axis, dim):
    count = lax.axis_size(axis)
    tiles = lax.all_to_all(split_up(array, dim, count), axis, 0, 0, tiled=True)
    return jnp.sum(tiles.astype(jnp.float32), axis=0)


def side_by_side(arrays, axis, dim, along):
    ends, at = ([], 0)
    for a in arrays[:-1]:
        at += a.shape[along]
        ends.append(at)
    both = jnp.concatenate(arrays, axis=along)
    return tuple(jnp.split(sent_and_summed(both, axis, dim), ends, axis=along))


def copy_for_each(array, axis):
    copies = jnp.broadcast_to(array, (lax.axis_size(axis), *array.shape))
    return lax.all_to_all(copies, axis, split_axis=0, concat_axis=0, tiled=True)


def in_order(tiles, dim):
    dims = list(tiles.shape[1:])
    dims[dim] *= tiles.shape[0]
    return jnp.moveaxis(tiles, 0, dim).reshape(dims)


def collect(array, axis, dim):
    tiles = copy_for_each(array, axis)
    return in_order(tiles, dim)


def layout(lengths, count):
    ending = jnp.cumsum(lengths)
    starts = ending - lengths
    places = jnp.arange(count, dtype=jnp.int32)
    owner = jnp.sum((places[:, None] >= ending[None, :]).astype(jnp.int32), axis=1)
    allowed = (owner[:, None] == owner[None, :]) & (places[:, None] >= places[None, :])
    return (owner, starts, allowed)


def head_grads(head_query, head_keys, head_values, head_cotangent, allowed):
    factor = HD ** (-0.5)
    scores = jnp.dot(head_query, head_keys.T, preferred_element_type=jnp.float32) * factor
    scores = jnp.where(allowed, scores, NEGATIVE)
    highest = jnp.max(scores, axis=1, keepdims=True)
    summed = jnp.sum(jnp.exp(scores - highest), axis=1, keepdims=True)
    chances = jnp.where(
        allowed, jnp.exp(scores - highest - jnp.log(summed)), jnp.zeros_like(scores)
    )
    slopes = jnp.dot(head_cotangent, head_values.T, preferred_element_type=jnp.float32)
    offsets = jnp.sum(chances * slopes, axis=1, keepdims=True)
    score_grads = (chances * (slopes - offsets)).astype(jnp.bfloat16)
    value_grads = jnp.dot(
        chances.astype(jnp.bfloat16).T, head_cotangent, preferred_element_type=jnp.float32
    )
    key_grads = jnp.dot(score_grads.T, head_query, preferred_element_type=jnp.float32) * factor
    return jnp.concatenate([key_grads, value_grads], axis=1)


def seq_fisher(inputs, grads_all, owner, starts, number_seqs):
    window = inputs.shape[0] // 2
    last_start = inputs.shape[0] - window

    def one_seq(running, number):
        opening = jnp.clip(starts[number], 0, last_start)
        rows_in = lax.dynamic_slice_in_dim(inputs, opening, window, 0)
        rows_grad = lax.dynamic_slice_in_dim(grads_all, opening, window, 0)
        inside = lax.dynamic_slice_in_dim(owner, opening, window, 0) == number
        rows_grad = jnp.where(inside[:, None], rows_grad, jnp.zeros_like(rows_grad))
        gradient = jnp.dot(rows_in.T, rows_grad, preferred_element_type=jnp.float32)
        return (running + gradient * gradient, None)

    start_value = jnp.zeros((inputs.shape[1], grads_all.shape[1]), jnp.float32)
    running, unused = lax.scan(one_seq, start_value, jnp.arange(number_seqs, dtype=jnp.int32))
    return running


def body(layer_inputs, queries, key_values, out_grads, lengths, task_weights):
    devices = lax.axis_size(COL)
    groups = devices // KVH
    pair_width = 2 * HD
    kv_width = key_values.shape[2]
    inputs = layer_inputs[0]
    count = inputs.shape[0]
    local_rows = key_values[0]
    copies = jnp.repeat(local_rows.reshape(local_rows.shape[0], KVH, pair_width), groups, axis=1)
    head_block = lax.all_to_all(copies, COL, split_axis=1, concat_axis=0, tiled=True).reshape(
        count, pair_width
    )
    owner, starts, allowed = layout(lengths[0], count)
    head_keys = head_block[:, :HD]
    head_values = head_block[:, HD:]
    local_queries = queries[0]
    local_cotangents = out_grads[0]
    partial_sum = jnp.zeros((count, pair_width), jnp.float32)
    for member in range(local_queries.shape[1] // HD):
        head_query = local_queries[:, member * HD : (member + 1) * HD]
        head_cotangent = local_cotangents[:, member * HD : (member + 1) * HD]
        partial_sum = partial_sum + head_grads(
            head_query, head_keys, head_values, head_cotangent, allowed
        )
    partial_value = partial_sum.astype(jnp.bfloat16)
    received = lax.all_to_all(
        partial_value.reshape(count, 1, pair_width), COL, split_axis=0, concat_axis=1, tiled=True
    )
    block_rows = received.shape[0]
    block_sums = jnp.sum(
        received.reshape(block_rows, KVH, groups, pair_width).astype(jnp.float32), axis=2
    )
    grads_all = gather_axes(block_sums.reshape(block_rows, kv_width).astype(jnp.bfloat16), COL, 0)
    fisher = seq_fisher(inputs, grads_all, owner, starts, lengths.shape[1])
    weighted = fisher * task_weights[0].astype(jnp.float32)
    weighted_sum, fisher_sum = side_by_side(
        (weighted.astype(jnp.bfloat16), fisher.astype(jnp.bfloat16)), "task", 0, 1
    )
    merged_part = (weighted_sum / (fisher_sum + EPS)).astype(jnp.bfloat16)
    merged = collect(merged_part, "task", 0)
    return (fisher[None], merged)


def solution(mesh):
    split = Mesh(mesh.devices.reshape(mesh.shape["task"], 8, 4), ("task", "col_0", "col_1"))
    placed = (
        P("task", None, COL),
        P("task", None, COL),
        P("task", COL, None),
        P("task", None, COL),
        P("task", None),
        P("task", COL, None),
    )
    return jax.shard_map(
        body,
        mesh=split,
        in_specs=placed,
        out_specs=(P("task", COL, None), P(COL, None)),
        check_vma=False,
    )
```

profile of v0, /device:TPU:1, one launch (start us, length us, event | category | flops | bytes accessed | tf_op | source)
XLA Modules:
  0.0 231.6 jit_solution(13057339239224431366)
XLA Ops:
  7.2 1.0 copy.20
  8.2 0.9 broadcast_in_dim.19
  9.1 11.9 %all-to-all-start = ((bf16[32,32,256]{2,0,1:T(8,128)(2,1)}), bf16[32,32,256]{2,0,1:T(8,128)(2,1)S(1)}, u32[]{:S(2)}, u32[]{:S(2)}) async-start(bf16[32,32,256]{2,0,1:T(8,128)(2,1)} %bitcast.5), calls=%async_computation | async-start | bytes 1048576 | tf_op jit(solution)/shard_map/all_to_all | solution.py:115
  21.0 0.8 reduce-window.8
  21.9 15.3 %all-to-all-done = bf16[32,32,256]{2,0,1:T(8,128)(2,1)S(1)} async-done(((bf16[32,32,256]{2,0,1:T(8,128)(2,1)}), bf16[32,32,256]{2,0,1:T(8,128)(2,1)S(1)}, u32[]{:S(2)}, u32[]{:S(2)}) %all-to-all-start) | async-done | bytes 524320 | tf_op jit(solution)/shard_map/all_to_all | solution.py:115
  37.2 1.7 fusion.45
  38.9 1.3 fusion.10
  40.2 3.0 %exponential_reduce_fusion = (f32[1024]{0:T(1024)S(1)}, f32[1024]{0:T(1024)S(1)}) fusion(f32[1024,1024]{0,1:T(8,128)S(1)} %get-tuple-element.86, f32[1024]{0:T(1024)S(1)} %get-tuple-element.68, s32[1024]{0:T(1024)S(1)} %convert_reduce_fusion.1, f32[1024]{0:T(1024)S(1)} %get-tuple-element.69, f32[1024,1024]{0,1:T(8,128)S(1)} %fusion.45), kind=kLoop, calls=%fused_computation.14 | loop fusion | flops 11532288 | bytes 8409088 | tf_op jit(solution)/shard_map/reduce_sum | solution.py:74
  43.2 0.7 fusion.40
  43.9 1.1 fusion.27
  45.1 1.1 fusion.24
  46.2 2.4 %multiply_reduce_fusion = (f32[1024]{0:T(1024)S(1)}, f32[1024]{0:T(1024)S(1)}, f32[1024,1024]{0,1:T(8,128)S(1)}) fusion(f32[1024]{0:T(1024)S(1)} %log.17, f32[1024]{0:T(1024)S(1)} %get-tuple-element.68, f32[1024,1024]{0,1:T(8,128)S(1)} %get-tuple-element.86, s32[1024]{0:T(1024)S(1)} %convert_reduce_fusion.1, f32[1024,1024]{0,1:T(8,128)S(1)} %fusion.40, ...), kind=kOutput, calls=%fused_computation.12 | convolution fusion | flops 286259200 | bytes 17334272 | tf_op jit(solution)/shard_map/dot_general | solution.py:78
  48.6 1.5 fusion.22
  50.2 1.5 fusion.23
  52.4 1.0 reduce.1
  53.8 20.3 %all_to_all.34 = bf16[32,2,4096]{2,1,0:T(2,128)(2,1)S(1)} all-to-all(bf16[32,2,4096]{2,1,0:T(2,128)(2,1)S(1)} %reshape.136), channel_id=1, replica_groups=mesh['task'=8,'col_0'=8,'col_1'=4] {'col_0','col_1'}, dimensions={0} | all-to-all | bytes 1048576 | tf_op jit(solution)/shard_map/all_to_all | solution.py:131
  74.9 11.2 %all_gather.6 = bf16[128,2048]{1,0:T(8,128)(2,1)} all-gather(bf16[32,2048]{1,0:T(8,128)(2,1)S(1)} %bitcast.52), channel_id=1, replica_groups=mesh['task'=8,'col_0'=8,'col_1'=4] {'col_1'}, dimensions={0}, use_global_device_ids=true | all-gather | bytes 655360 | tf_op jit(solution)/shard_map/all_gather | solution.py:19
  86.1 56.2 %all-gather.2.cloned.1.call-done = bf16[1024,2048]{1,0:T(8,128)(2,1)} async-done(((bf16[128,2048]{1,0:T(8,128)(2,1)}), bf16[1024,2048]{1,0:T(8,128)(2,1)}) %all-gather.2.cloned.1.call-update) | async-done | bytes 4194320 | tf_op jit(solution)/shard_map/all_gather | solution.py:19
  142.3 30.2 %while.11 = (s32[]{:T(128)}, f32[256,2048]{1,0:T(8,128)S(1)}, s32[4]{0:T(128)S(1)}, s32[4]{0:T(128)S(1)}, bf16[1024,256]{1,0:T(8,128)(2,1)}, /*index=5*/s32[1024...) while((s32[]{:T(128)}, f32[256,2048]{1,0:T(8,128)S(1)}, ...), condition=%wide.region_10.11_spmd.clone, body=%wide.region_9.10_spmd.clone.sunk | while | flops 539492864 | bytes 6557913 | solution.py:102
  144.9 0.6 dynamic_slice.37
  146.1 0.7 dynamic-slice_compare_fusion.2
  146.8 3.1 %fusion.66 = f32[256,2048]{1,0:T(8,128)S(1)} fusion(f32[256,2048]{1,0:T(8,128)S(1)} %get-tuple-element.144, bf16[1024,2048]{1,0:T(8,128)(2,1)} %get-tuple-element.161, s32[]{:T(128)} %bitcast.43, pred[512]{0:T(512)(128)(4,1)S(1)} %dynamic-slice_compare_fusion.2, pred[]{:T(512)S(6)} %compare.3, bf16[1024,256]{1,0:T(8,128)(2,1)} %get-tuple-element.159), kind=kOutput, calls=%fused_computation.1.clone.1 | convolution fusion | flops 539492352 | bytes 6555137 | tf_op jit(solution)/shard_map/while/body/eval_jaxpr/dot_general | solution.py:98
  153.6 0.7 dynamic-slice_compare_fusion.2
  154.4 3.1 %fusion.66 = f32[256,2048]{1,0:T(8,128)S(1)} fusion(f32[256,2048]{1,0:T(8,128)S(1)} %get-tuple-element.144, bf16[1024,2048]{1,0:T(8,128)(2,1)} %get-tuple-element.161, s32[]{:T(128)} %bitcast.43, pred[512]{0:T(512)(128)(4,1)S(1)} %dynamic-slice_compare_fusion.2, pred[]{:T(512)S(6)} %compare.3, bf16[1024,256]{1,0:T(8,128)(2,1)} %get-tuple-element.159), kind=kOutput, calls=%fused_computation.1.clone.1 | convolution fusion | flops 539492352 | bytes 6555137 | tf_op jit(solution)/shard_map/while/body/eval_jaxpr/dot_general | solution.py:98
  161.2 0.7 dynamic-slice_compare_fusion.2
  161.9 3.1 %fusion.66 = f32[256,2048]{1,0:T(8,128)S(1)} fusion(f32[256,2048]{1,0:T(8,128)S(1)} %get-tuple-element.144, bf16[1024,2048]{1,0:T(8,128)(2,1)} %get-tuple-element.161, s32[]{:T(128)} %bitcast.43, pred[512]{0:T(512)(128)(4,1)S(1)} %dynamic-slice_compare_fusion.2, pred[]{:T(512)S(6)} %compare.3, bf16[1024,256]{1,0:T(8,128)(2,1)} %get-tuple-element.159), kind=kOutput, calls=%fused_computation.1.clone.1 | convolution fusion | flops 539492352 | bytes 6555137 | tf_op jit(solution)/shard_map/while/body/eval_jaxpr/dot_general | solution.py:98
  168.8 0.7 dynamic-slice_compare_fusion.2
  169.5 3.0 %fusion.66 = f32[256,2048]{1,0:T(8,128)S(1)} fusion(f32[256,2048]{1,0:T(8,128)S(1)} %get-tuple-element.144, bf16[1024,2048]{1,0:T(8,128)(2,1)} %get-tuple-element.161, s32[]{:T(128)} %bitcast.43, pred[512]{0:T(512)(128)(4,1)S(1)} %dynamic-slice_compare_fusion.2, pred[]{:T(512)S(6)} %compare.3, bf16[1024,256]{1,0:T(8,128)(2,1)} %get-tuple-element.159), kind=kOutput, calls=%fused_computation.1.clone.1 | convolution fusion | flops 539492352 | bytes 6555137 | tf_op jit(solution)/shard_map/while/body/eval_jaxpr/dot_general | solution.py:98
  173.2 0.6 copy-done
  173.9 31.1 %all_to_all.35 = bf16[8,32,4096]{2,1,0:T(8,128)(2,1)S(1)} all-to-all(bf16[8,32,4096]{2,1,0:T(8,128)(2,1)S(1)} %bitcast.44), channel_id=1, replica_groups=mesh['task'=8,'col_0'=8,'col_1'=4] {'task'}, dimensions={0} | all-to-all | bytes 4194304 | tf_op jit(solution)/shard_map/all_to_all | solution.py:31
  205.4 18.4 %all_to_all.36 = bf16[8,32,2048]{2,1,0:T(8,128)(2,1)S(1)} all-to-all(bf16[8,32,2048]{2,1,0:T(8,128)(2,1)S(1)} %broadcast_in_dim.42), channel_id=1, replica_groups=mesh['task'=8,'col_0'=8,'col_1'=4] {'task'}, dimensions={0} | all-to-all | bytes 2097152 | tf_op jit(solution)/shard_map/all_to_all | solution.py:46
  223.8 1.0 copy.29
  (38 shorter events, 7.2 us)
Async XLA Ops:
  7.2 31.7 %copy-start.3 = (bf16[1,1024,256]{2,1,0:T(8,128)(2,1)S(1)}, bf16[1,1024,256]{2,1,0:T(8,128)(2,1)}, u32[]{:S(2)}) copy-start(bf16[1,1024,256]{2,1,0:T(8,128)(2,1)} %param.9) | copy-start | bytes 1572868
  9.1 28.1 %all-to-all-start = ((bf16[32,32,256]{2,0,1:T(8,128)(2,1)}), bf16[32,32,256]{2,0,1:T(8,128)(2,1)S(1)}, u32[]{:S(2)}, u32[]{:S(2)}) async-start(bf16[32,32,256]{2,0,1:T(8,128)(2,1)} %bitcast.5), calls=%async_computation | async-start | bytes 1048576 | tf_op jit(solution)/shard_map/all_to_all | solution.py:115
  20.9 121.4 %all-gather.2.cloned.1.call-start = ((), (), s32[]{:S(2)}) async-start(), calls=%async_computation.4 | async-start | bytes 4718592 | tf_op jit(solution)/shard_map/all_gather | solution.py:19
  40.2 3.0 %copy-start.2 = (bf16[1,1024,256]{2,1,0:T(8,128)(2,1)S(1)}, bf16[1,1024,256]{2,1,0:T(8,128)(2,1)}, u32[]{:S(2)}) copy-start(bf16[1,1024,256]{2,1,0:T(8,128)(2,1)} %param.11) | copy-start | bytes 1572868
  53.5 32.7 %copy-start.4 = (s32[1,4]{1,0:T(1,128)S(1)}, s32[1,4]{1,0:T(1,128)}, u32[]{:S(2)}) copy-start(s32[1,4]{1,0:T(1,128)} %param.12) | copy-start | bytes 52
  142.3 30.2 %copy-start.1 = (bf16[1,256,2048]{2,1,0:T(8,128)(2,1)S(1)}, bf16[1,256,2048]{2,1,0:T(8,128)(2,1)}, u32[]{:S(2)}) copy-start(bf16[1,256,2048]{2,1,0:T(8,128)(2,1)} %param.13) | copy-start | bytes 3145732
  172.5 1.3 copy-start
Sparse Core Ops, SparseCore 0:
  86.2 56.0 all-gather.1
where the time goes:
time: 232 us
  blocking collectives  81 us (35%)
  waiting for transfers between devices  71.5 us (31%)
  matrix products  23.6 us (10%)
  between operations  14.3 us (6%)
  starting transfers between devices  11.9 us (5%)
  loops' own time  10.4 us (4%)
  local copies, waits for them, and re-layouts  9.8 us (4%)
  other arithmetic  9.14 us (4%)
    all_gather x1, waiting for transfers between devices, gather_axes(): nearer = lax.all_gather(array, axes[-1], axis=dim, tiled=True)  56.2 us
    all_to_all x1, blocking collectives, sent_and_summed(): tiles = lax.all_to_all(split_up(array, dim, count), axis, 0, 0, tiled=True)  31.1 us
    all_to_all x1, blocking collectives, body(): lax.all_to_all(partial_value.reshape(count, 1, pair_width), COL, split_ax...  20.3 us
    all_to_all x1, blocking collectives, copy_for_each(): return lax.all_to_all(copies, axis, split_axis=0, concat_axis=0, tiled=True)  18.4 us
    all_to_all x1, waiting for transfers between devices, body(): lax.all_to_all(copies, COL, split_axis=1, concat_axis=0, tiled=True)  15.3 us
    dot_general x4, matrix products, one_seq(): gradient = jnp.dot(rows_in.T, rows_grad, preferred_element_type=jnp.float32)  12.2 us
    all_to_all x1, starting transfers between devices, body(): lax.all_to_all(copies, COL, split_axis=1, concat_axis=0, tiled=True)  11.9 us
    all_gather x1, blocking collectives, gather_axes(): nearer = lax.all_gather(array, axes[-1], axis=dim, tiled=True)  11.2 us
  transfers between devices with their start and end apart: 2, of which 2 were waited for; matrix products, arithmetic and copies ran while one was open for 0% of the time, Pallas kernels for 0%

commit v1 on v0

v1 whole, which is shorter than its diff:
```python
import functools

import jax
import jax.numpy as jnp
from jax import lax
from jax.experimental import pallas as pl
from jax.experimental.pallas import tpu as pltpu
from jax.sharding import PartitionSpec as P

MESH = pl.DeviceIdType.MESH
F32, BF16 = jnp.float32, jnp.bfloat16
KVH = 8
HD = 128
PAIR = 2 * HD
TOK = 1024
BLK = 256
CUT = 96
REST = BLK - CUT
EPS = 1e-06
NEGATIVE = -1e30


class Where:
    def __init__(self):
        self.task, self.col = lax.axis_index("task"), lax.axis_index("col")
        self.y, self.core = self.task // 2, self.task % 2
        self.z, self.x = self.col // 4, self.col % 4

    def along_x(self, by):
        return (self.task, self.z * 4 + (self.x + by + 4) % 4)

    def along_z(self, by):
        return (self.task, ((self.z + by + 8) % 8) * 4 + self.x)

    def along_y(self, by):
        return (((self.y + by) % 4) * 2 + self.core, self.col)

    def other_core(self):
        return (self.y * 2 + 1 - self.core, self.col)


def meet(devices):
    barrier = pltpu.get_barrier_semaphore()
    for device in devices:
        pl.semaphore_signal(barrier, inc=1, device_id=device, device_id_type=MESH)
    pl.semaphore_wait(barrier, len(devices))


class Sender:
    def __init__(self, send_sems, recv_sems):
        self.send_sems, self.recv_sems, self.copies = send_sems, recv_sems, []

    def start(self, src, dst, device):
        at = len(self.copies)
        copy = pltpu.make_async_remote_copy(
            src_ref=src,
            dst_ref=dst,
            send_sem=self.send_sems.at[at],
            recv_sem=self.recv_sems.at[at],
            device_id=device,
            device_id_type=MESH,
        )
        copy.start()
        self.copies.append(copy)
        return copy

    def finish(self):
        for copy in self.copies:
            copy.wait_send()


def bounds(lengths_ref):
    ends, end = [], 0
    for s in range(4):
        end = end + lengths_ref[0, s]
        ends.append(end)
    return ends


def dot_nt(a, b):
    return lax.dot_general(a, b, (((1,), (1,)), ((), ())), preferred_element_type=F32)


def grads_kernel(
    kv_ref, q_ref, og_ref, len_ref, out_ref, kv, score, slope, acc, send_sems, recv_sems, own_sem
):
    at = Where()
    send = Sender(send_sems, recv_sems)
    meet([at.along_x(1), at.along_x(-1)] + [at.along_z(k) for k in range(1, 8)])

    def rows(z, x):
        return pl.ds(pl.multiple_of(z * 128 + x * 32, 32), 32)

    def half(z, x, part):
        return pl.ds(pl.multiple_of(z * 128 + x * 32 + part * 16, 16), 16)

    def head(h):
        return pl.ds(pl.multiple_of(h * PAIR, PAIR), PAIR)

    own = pltpu.make_async_copy(kv_ref.at[:, head(at.z)], kv.at[rows(at.z, at.x)], own_sem)
    own.start()
    steps = (1, 7, 2, 6, 3, 5, 4)
    arrive = {}
    for k in steps:
        arrive[k] = send.start(
            kv_ref.at[:, head((at.z + k) % 8)], kv.at[rows(at.z, at.x)], at.along_z(k)
        )
    own.wait()
    first, second = [], []

    def spread(z):
        block = kv.at[rows(z, at.x)]
        first.append((z, send.start(block, block, at.along_x(1)), send.start(block, block, at.along_x(-1))))

    def pass_on():
        z, up, down = first.pop(0)
        up.wait_recv()
        block = kv.at[half(z, (at.x + 3) % 4, 0)]
        second.append(send.start(block, block, at.along_x(1)))
        down.wait_recv()
        block = kv.at[half(z, (at.x + 1) % 4, 1)]
        second.append(send.start(block, block, at.along_x(-1)))

    spread(at.z)
    for n, k in enumerate(steps):
        arrive[k].wait_recv()
        spread((at.z + 8 - k) % 8)
        if n >= 1:
            pass_on()
    while first:
        pass_on()
    for copy in second:
        copy.wait_recv()

    factor = HD**-0.5
    ends = bounds(len_ref)
    blocks = TOK // BLK
    for i in reversed(range(blocks)):
        queries = pl.ds(i * BLK, BLK)
        low = max(0, i - 2)
        token = i * BLK + lax.broadcasted_iota(jnp.int32, (1, BLK), 1)
        opening = jnp.zeros_like(token)
        for s in range(3):
            opening = jnp.where(token >= ends[s], ends[s], opening)
        for m in range(2):
            lanes = pl.ds(m * HD, HD)
            query = q_ref[queries, lanes]
            cot = og_ref[queries, lanes]
            highest = jnp.full((1, BLK), NEGATIVE, F32)
            for j in range(low, i + 1):
                key = kv[pl.ds(j * BLK, BLK), 0:HD]
                place = j * BLK + lax.broadcasted_iota(jnp.int32, (BLK, BLK), 0)
                allowed = place >= opening
                if j == i:
                    allowed = allowed & (place <= token)
                s = jnp.where(allowed, dot_nt(key, query) * factor, NEGATIVE)
                score[j - low] = s
                highest = jnp.maximum(highest, jnp.max(s, axis=0, keepdims=True))
            total = jnp.zeros((1, BLK), F32)
            weighed = jnp.zeros((1, BLK), F32)
            for j in range(low, i + 1):
                e = jnp.exp(score[j - low] - highest)
                score[j - low] = e
                d = dot_nt(kv[pl.ds(j * BLK, BLK), HD:PAIR], cot)
                slope[j - low] = d
                total = total + jnp.sum(e, axis=0, keepdims=True)
                weighed = weighed + jnp.sum(e * d, axis=0, keepdims=True)
            inverse = 1.0 / total
            offset = weighed * inverse
            for j in range(low, i + 1):
                p = score[j - low] * inverse
                ds = (p * (slope[j - low] - offset)).astype(BF16)
                to = pl.ds(j * BLK, BLK)
                dk = jnp.dot(ds, query, preferred_element_type=F32)
                dv = jnp.dot(p.astype(BF16), cot, preferred_element_type=F32)
                if m == 0 and i == min(blocks - 1, j + 2):
                    acc[to, 0:HD] = dk
                    acc[to, HD:PAIR] = dv
                else:
                    acc[to, 0:HD] += dk
                    acc[to, HD:PAIR] += dv
        done = pl.ds(i * BLK, BLK)
        out_ref[done, 0:HD] = (acc[done, 0:HD] * factor).astype(BF16)
        out_ref[done, HD:PAIR] = acc[done, HD:PAIR].astype(BF16)
    send.finish()


def merge_kernel(
    p_ref,
    x_ref,
    w_ref,
    len_ref,
    fisher_out,
    merged_out,
    xm,
    g,
    half_in,
    half_out,
    fb,
    ps,
    pr,
    ys,
    yr,
    mb,
    send_sems,
    recv_sems,
    out_sems,
):
    at = Where()
    send = Sender(send_sems, recv_sems)
    x, z, y, core = at.x, at.z, at.y, at.core
    meet(
        [at.along_x(1), at.along_x(-1), at.along_z(1), at.along_z(-1), at.other_core()]
        + [at.along_y(k) for k in (1, 2, 3)]
    )

    def quarter(by, part):
        return p_ref.at[
            pl.ds(pl.multiple_of(((x + by + 4) % 4) * BLK, BLK), BLK), part * HD : part * HD + HD
        ]

    far_k = send.start(quarter(2, 0), half_in.at[0], at.along_x(1))
    far_v = send.start(quarter(2, 1), half_in.at[1], at.along_x(-1))
    near_v = send.start(quarter(1, 1), half_in.at[2], at.along_x(1))
    near_k = send.start(quarter(-1, 0), half_in.at[3], at.along_x(-1))

    ends = bounds(len_ref)
    starts = [0] + ends[:3]
    for hf in range(2):
        o = 2 * BLK * hf
        rows = jnp.concatenate(
            [
                x_ref[o : o + CUT],
                x_ref[o + BLK : o + BLK + CUT],
                x_ref[o + CUT : o + BLK],
                x_ref[o + BLK + CUT : o + 2 * BLK],
            ],
            axis=0,
        )
        turned = rows.T
        pos = lax.broadcasted_iota(jnp.int32, (1, 2 * BLK), 1)
        late = pos - 2 * CUT
        token = o + jnp.where(
            pos < 2 * CUT,
            pos + jnp.where(pos >= CUT, BLK - CUT, 0),
            late + CUT + jnp.where(late >= REST, BLK - REST, 0),
        )
        for n in range(3):
            s = hf + n
            inside = jnp.where((token >= starts[s]) & (token < ends[s]), 1.0, 0.0).astype(BF16)
            masked = turned * inside
            for rb in range(2):
                xm[rb, hf, n * HD : (n + 1) * HD, :] = masked[rb * HD : (rb + 1) * HD]

    far_k.wait_recv()
    half_out[0] = (quarter(1, 0)[...].astype(F32) + half_in[0].astype(F32)).astype(BF16)
    sum_k = send.start(half_out.at[0], half_in.at[4], at.along_x(1))
    far_v.wait_recv()
    half_out[1] = (quarter(-1, 1)[...].astype(F32) + half_in[1].astype(F32)).astype(BF16)
    sum_v = send.start(half_out.at[1], half_in.at[5], at.along_x(-1))

    def cut_rows(q):
        return (q // 2, pl.ds(pl.multiple_of(CUT * (q % 2), CUT), CUT))

    def rest_rows(q):
        return (q // 2, pl.ds(pl.multiple_of(2 * CUT + REST * (q % 2), 32), REST))

    def settle(part, near, through):
        own = quarter(0, part)[...].astype(F32) + half_in[near].astype(F32) + half_in[through].astype(F32)
        own = own.astype(BF16)
        lanes = slice(part * HD, part * HD + HD)
        hf, r = cut_rows(x)
        g[z, hf, r, lanes] = own[:CUT]
        hf, r = rest_rows(x)
        g[z, hf, r, lanes] = own[CUT:]

    near_k.wait_recv()
    sum_k.wait_recv()
    settle(0, 3, 4)
    near_v.wait_recv()
    sum_v.wait_recv()
    settle(1, 2, 5)

    def ring_piece(h, place, base, size, part):
        q = (x + place) % 4
        unit = size // 2
        length = size if part is None else unit
        skip = 0 if part is None else part * unit
        start = pl.multiple_of(base + size * (q % 2) + skip, 16)
        return g.at[h, q // 2, pl.ds(start, length)]

    class AroundX:
        def __init__(self, h, base, size):
            self.h, self.base, self.size = h, base, size
            own = ring_piece(h, 0, base, size, None)
            self.up = send.start(own, own, at.along_x(1))
            self.down = send.start(own, own, at.along_x(-1))

        def pass_on(self):
            self.up.wait_recv()
            piece = ring_piece(self.h, 3, self.base, self.size, 0)
            self.up2 = send.start(piece, piece, at.along_x(1))
            self.down.wait_recv()
            piece = ring_piece(self.h, 1, self.base, self.size, 1)
            self.down2 = send.start(piece, piece, at.along_x(-1))

        def end(self):
            self.up2.wait_recv()
            self.down2.wait_recv()

    def head(k):
        return (z + k + 8) % 8

    def send_rest(h, way):
        hf, r = rest_rows(x)
        piece = g.at[h, hf, r]
        return send.start(piece, piece, at.along_z(way))

    def send_cut(h, hf, way):
        piece = g.at[h, hf, 0 : 2 * CUT]
        return send.start(piece, piece, at.along_z(way))

    outs = []

    def columns(h):
        return pl.ds(pl.multiple_of(h * PAIR, PAIR), PAIR)

    def fisher_rows(slot, h, rb):
        a = jnp.dot(xm[rb, 0], g[h, 0], preferred_element_type=F32)
        b = jnp.dot(xm[rb, 1], g[h, 1], preferred_element_type=F32)
        g0, g3 = a[:HD], b[2 * HD :]
        g1, g2 = a[HD : 2 * HD] + b[:HD], a[2 * HD :] + b[HD : 2 * HD]
        f = g0 * g0 + g1 * g1 + g2 * g2 + g3 * g3
        fb[slot, pl.ds(pl.multiple_of(rb * HD, HD), HD), :] = f
        return f

    def weights(h, rb):
        return w_ref[pl.ds(pl.multiple_of(rb * HD, HD), HD), columns(h)].astype(F32)

    pair, over_y, merged_y, merged_core = {}, {}, {}, {}
    heads = [0, -1, 1, -2, 2, -3, 3, 4]

    def compute_other(slot):
        h = head(heads[slot])
        rb = 1 - core
        f = fisher_rows(slot, h, rb)
        ps[slot, 0] = (f * weights(h, rb)).astype(BF16)
        ps[slot, 1] = f.astype(BF16)
        pair[slot] = send.start(ps.at[slot], pr.at[slot], at.other_core())

    def compute_own(slot):
        h = head(heads[slot])
        fisher_rows(slot, h, core)
        copy = pltpu.make_async_copy(fb.at[slot], fisher_out.at[:, columns(h)], out_sems.at[slot])
        copy.start()
        outs.append(copy)

    def sum_pair(slot):
        h = head(heads[slot])
        pair[slot].wait_recv()
        f = fb[slot, pl.ds(pl.multiple_of(core * HD, HD), HD), :]
        ys[slot, 0] = (f * weights(h, core) + pr[slot, 0].astype(F32)).astype(BF16)
        ys[slot, 1] = (f + pr[slot, 1].astype(F32)).astype(BF16)
        over_y[slot] = []
        for k in (2, 1, 3):
            rows = pl.ds(pl.multiple_of(((y + k) % 4) * 32, 32), 32)
            over_y[slot].append(send.start(ys.at[slot, :, rows], yr.at[slot, k - 1], at.along_y(k)))

    def divide(slot):
        h = head(heads[slot])
        for copy in over_y[slot]:
            copy.wait_recv()
        rows = pl.ds(pl.multiple_of(y * 32, 32), 32)
        sums = ys[slot, :, rows, :].astype(F32)
        for k in range(3):
            sums = sums + yr[slot, k].astype(F32)
        to = pl.ds(pl.multiple_of(core * HD + y * 32, 32), 32)
        mb[h, to, :] = (sums[0] / (sums[1] + EPS)).astype(BF16)
        piece = mb.at[h, to]
        merged_y[slot] = [send.start(piece, piece, at.along_y(k)) for k in (2, 1, 3)]

    def share(slot):
        h = head(heads[slot])
        for copy in merged_y[slot]:
            copy.wait_recv()
        piece = mb.at[h, pl.ds(pl.multiple_of(core * HD, HD), HD)]
        merged_core[slot] = send.start(piece, piece, at.other_core())

    def close(slot):
        h = head(heads[slot])
        merged_core[slot].wait_recv()
        copy = pltpu.make_async_copy(mb.at[h], merged_out.at[:, columns(h)], out_sems.at[8 + slot])
        copy.start()
        outs.append(copy)

    stages = (sum_pair, divide, share, close)
    progress = {s: 0 for s in range(8)}

    def advance(upto):
        for slot in range(upto):
            if progress[slot] < len(stages):
                stages[progress[slot]](slot)
                progress[slot] += 1

    rest_up = send_rest(z, 1)
    rest_down = send_rest(z, -1)
    cut_ring = AroundX(z, 0, CUT)
    rings = [AroundX(z, 2 * CUT, REST)]
    cut_ring.pass_on()
    cut_ring.end()
    up0, down0 = send_cut(z, 0, 1), send_cut(z, 0, -1)
    up1, down1 = send_cut(z, 1, 1), send_cut(z, 1, -1)
    rings[0].pass_on()
    rings[0].end()
    ready = [0]

    for k in range(1, 5):
        above, below = head(-k), head(k)
        rings = []
        if k < 4:
            rest_up.wait_recv()
            rings.append(AroundX(above, 2 * CUT, REST))
            if k < 3:
                rest_up, up_old = send_rest(above, 1), rest_up
        rest_down.wait_recv()
        rings.append(AroundX(below, 2 * CUT, REST))
        if k < 4:
            rest_down = send_rest(below, -1)
        if k == 3:
            rest_up = None
        work = []
        for slot in ready:
            work += [functools.partial(compute_other, slot), functools.partial(compute_own, slot)]
        done = ready[-1] + 1

        def next_work():
            if work:
                work.pop(0)()

        next_work()
        up0.wait_recv()
        if k < 4:
            up0 = send_cut(above, 0, 1)
            down0.wait_recv()
            if k < 3:
                down0 = send_cut(below, 0, -1)
        next_work()
        for ring in rings:
            ring.pass_on()
        next_work()
        if k < 4:
            up1.wait_recv()
            if k < 3:
                up1 = send_cut(above, 1, 1)
        down1.wait_recv()
        if k < 4:
            down1 = send_cut(below, 1, -1)
        next_work()
        for ring in rings:
            ring.end()
        advance(done)
        ready = [2 * k - 1, 2 * k] if k < 4 else [7]

    compute_other(7)
    compute_own(7)
    while any(progress[s] < len(stages) for s in range(8)):
        advance(8)
    send.finish()
    for copy in outs:
        copy.wait()


def vmem():
    return pl.BlockSpec(memory_space=pltpu.VMEM)


def body(layer_inputs, queries, key_values, out_grads, lengths, task_weights):
    smem = pl.BlockSpec(memory_space=pltpu.SMEM)
    partial = pl.pallas_call(
        grads_kernel,
        out_shape=jax.ShapeDtypeStruct((TOK, PAIR), BF16),
        in_specs=[vmem(), vmem(), vmem(), smem],
        out_specs=vmem(),
        scratch_shapes=[
            pltpu.VMEM((TOK, PAIR), BF16),
            pltpu.VMEM((3, BLK, BLK), F32),
            pltpu.VMEM((3, BLK, BLK), F32),
            pltpu.VMEM((TOK, PAIR), F32),
            pltpu.SemaphoreType.DMA((39,)),
            pltpu.SemaphoreType.DMA((39,)),
            pltpu.SemaphoreType.DMA,
        ],
        compiler_params=pltpu.CompilerParams(collective_id=0, has_side_effects=True),
        name="grads",
    )(key_values[0], queries[0], out_grads[0], lengths)
    fisher, merged = pl.pallas_call(
        merge_kernel,
        out_shape=(
            jax.ShapeDtypeStruct((BLK, KVH * PAIR), F32),
            jax.ShapeDtypeStruct((BLK, KVH * PAIR), BF16),
        ),
        in_specs=[vmem(), vmem(), vmem(), smem],
        out_specs=(pl.BlockSpec(memory_space=pl.ANY), pl.BlockSpec(memory_space=pl.ANY)),
        scratch_shapes=[
            pltpu.VMEM((2, 2, 3 * HD, 2 * BLK), BF16),
            pltpu.VMEM((KVH, 2, 2 * BLK, PAIR), BF16),
            pltpu.VMEM((6, BLK, HD), BF16),
            pltpu.VMEM((2, BLK, HD), BF16),
            pltpu.VMEM((8, BLK, PAIR), F32),
            pltpu.VMEM((8, 2, HD, PAIR), BF16),
            pltpu.VMEM((8, 2, HD, PAIR), BF16),
            pltpu.VMEM((8, 2, HD, PAIR), BF16),
            pltpu.VMEM((8, 3, 2, 32, PAIR), BF16),
            pltpu.VMEM((KVH, BLK, PAIR), BF16),
            pltpu.SemaphoreType.DMA((132,)),
            pltpu.SemaphoreType.DMA((132,)),
            pltpu.SemaphoreType.DMA((16,)),
        ],
        compiler_params=pltpu.CompilerParams(collective_id=1, has_side_effects=True),
        name="merge",
    )(partial, layer_inputs[0], task_weights[0], lengths)
    return fisher[None], merged


def solution(mesh):
    placed = (
        P("task", None, "col"),
        P("task", None, "col"),
        P("task", "col", None),
        P("task", None, "col"),
        P("task", None),
        P("task", "col", None),
    )
    return jax.shard_map(
        body,
        mesh=mesh,
        in_specs=placed,
        out_specs=(P("task", "col", None), P("col", None)),
        check_vma=False,
    )
```

time: 232 us -> 114 us (0.49)
  Pallas kernels: 0 us -> 109 us
  blocking collectives: 81 us -> 0 us
  waiting for transfers between devices: 71.5 us -> 0 us
  matrix products: 23.6 us -> 0 us
  between operations: 14.3 us -> 0.66 us
  starting transfers between devices: 11.9 us -> 0 us
  loops' own time: 10.4 us -> 0 us
  other arithmetic: 9.14 us -> 0 us
  local copies, waits for them, and re-layouts: 9.8 us -> 4.2 us
    pallas_call x0 -> x2, Pallas kernels: none -> 109 us  [the longest x1 81.3 us: body(): pl.pallas_call(merge_kernel, out_shape=(jax.ShapeDtypeStruct((BLK, KVH *...]
    all_to_all x3 -> x0, blocking collectives: 69.8 us -> none  [the longest x1 31.1 us: sent_and_summed(): tiles = lax.all_to_all(split_up(array, dim, count), axis, 0, 0, tiled=True)]
    all_gather x1 -> x0, waiting for transfers between devices: 56.2 us -> none  [gather_axes(): nearer = lax.all_gather(array, axes[-1], axis=dim, tiled=True)]
    dot_general x12 -> x0, matrix products: 23.6 us -> none  [the longest x4 12.2 us: one_seq(): gradient = jnp.dot(rows_in.T, rows_grad, preferred_element_type=jnp.float32)]
    all_to_all x1 -> x0, waiting for transfers between devices: 15.3 us -> none  [body(): lax.all_to_all(copies, COL, split_axis=1, concat_axis=0, tiled=True)]
    all_to_all x1 -> x0, starting transfers between devices: 11.9 us -> none  [body(): lax.all_to_all(copies, COL, split_axis=1, concat_axis=0, tiled=True)]
    all_gather x1 -> x0, blocking collectives: 11.2 us -> none  [gather_axes(): nearer = lax.all_gather(array, axes[-1], axis=dim, tiled=True)]
    another operation x1 -> x0, loops' own time: 10.4 us -> none  [seq_fisher(): lax.scan(one_seq, start_value, jnp.arange(number_seqs, dtype=jnp.int32))]
  transfers between devices with their start and end apart: 2 -> 0, of which waited for: 2 -> 0; matrix products, arithmetic and copies ran while one was open for 0% -> 0% of each run, Pallas kernels for 0% -> 0%
where the time goes in v1:
time: 114 us
  Pallas kernels  109 us (96%)
  local copies, waits for them, and re-layouts  4.2 us (4%)
    pallas_call x1, Pallas kernels, body(): pl.pallas_call(merge_kernel, out_shape=(jax.ShapeDtypeStruct((BLK, KVH *...  81.3 us
    pallas_call x1, Pallas kernels, body(): pl.pallas_call(grads_kernel, out_shape=jax.ShapeDtypeStruct((TOK, PAIR),...  27.6 us
    unnamed x4, local copies, waits for them, and re-layouts  4.2 us

profile of v1, /device:TPU:1, one launch (start us, length us, event | category | flops | bytes accessed | tf_op | source)
XLA Modules:
  0.0 113.7 jit_solution(3363777647105054935)
XLA Ops:
  0.6 27.6 %grads.1.p_ref = bf16[1024,256]{1,0:T(8,128)(2,1)} custom-call(bf16[32,2048]{1,0:T(8,128)(2,1)} %bitcast.11, bf16[1024,256]{1,0:T(8,128)(2,1)} %bitcast.9, bf16[1024,256]{1,0:T(8,128)(2,1)} %bitcast.10, s32[1,4]{1,0:T(1,128)} %len_ref.3), custom_call_target="tpu_custom_call" | custom-call | tf_op jit(solution)/shard_map/grads/pallas_call | solution.py:479
  28.2 81.3 %merge.1 = (f32[256,2048]{1,0:T(8,128)}, bf16[256,2048]{1,0:T(8,128)(2,1)}) custom-call(bf16[1024,256]{1,0:T(8,128)(2,1)} %grads.1.p_ref, bf16[1024,256]{1,0:T(8,128)(2,1)} %bitcast.8, bf16[256,2048]{1,0:T(8,128)(2,1)} %bitcast.7, s32[1,4]{1,0:T(1,128)} %len_ref.3), custom_call_target="tpu_custom_call" | custom-call | tf_op jit(solution)/shard_map/merge/pallas_call | solution.py:496
  109.5 0.0 copy-start
  109.5 3.2 %copy.10 = f32[1,256,2048]{2,1,0:T(8,128)} copy(f32[1,256,2048]{2,1,0:T(8,128)} %bitcast.6) | data formatting | bytes 4194304
  112.7 0.0 copy-done
  112.7 1.0 copy.11
Async XLA Ops:
  109.5 3.2 %copy-start = (bf16[256,2048]{1,0:T(8,128)(2,1)S(1)}, bf16[256,2048]{1,0:T(8,128)(2,1)}, u32[]{:S(2)}) copy-start(bf16[256,2048]{1,0:T(8,128)(2,1)} %get-tuple-element.9) | copy-start | bytes 3145732

commit v2 on v1

v2 whole, which is shorter than its diff:
```python
import functools

import jax
import jax.numpy as jnp
from jax import lax
from jax.experimental import pallas as pl
from jax.experimental.pallas import tpu as pltpu
from jax.sharding import PartitionSpec as P

MESH = pl.DeviceIdType.MESH
F32, BF16 = jnp.float32, jnp.bfloat16
KVH = 8
HD = 128
PAIR = 2 * HD
TOK = 1024
BLK = 256
CUT = 96
REST = BLK - CUT
EPS = 1e-06
NEGATIVE = -1e30
SEMS = 164


class Where:
    def __init__(self):
        self.task, self.col = lax.axis_index("task"), lax.axis_index("col")
        self.y, self.core = self.task // 2, self.task % 2
        self.z, self.x = self.col // 4, self.col % 4

    def along_x(self, by):
        return (self.task, self.z * 4 + (self.x + by + 4) % 4)

    def along_z(self, by):
        return (self.task, ((self.z + by + 8) % 8) * 4 + self.x)

    def along_y(self, by, across=False):
        core = 1 - self.core if across else self.core
        return (((self.y + by) % 4) * 2 + core, self.col)

    def other_core(self):
        return (self.y * 2 + 1 - self.core, self.col)


def meet(devices):
    barrier = pltpu.get_barrier_semaphore()
    for device in devices:
        pl.semaphore_signal(barrier, inc=1, device_id=device, device_id_type=MESH)
    pl.semaphore_wait(barrier, len(devices))


class Sender:
    def __init__(self, send_sems, recv_sems):
        self.send_sems, self.recv_sems, self.copies = send_sems, recv_sems, []

    def start(self, src, dst, device):
        at = len(self.copies)
        copy = pltpu.make_async_remote_copy(
            src_ref=src,
            dst_ref=dst,
            send_sem=self.send_sems.at[at],
            recv_sem=self.recv_sems.at[at],
            device_id=device,
            device_id_type=MESH,
        )
        copy.start()
        self.copies.append(copy)
        return copy

    def finish(self):
        for copy in self.copies:
            copy.wait_send()


def bounds(lengths_ref):
    ends, end = [], 0
    for s in range(4):
        end = end + lengths_ref[0, s]
        ends.append(end)
    return ends


def dot_nt(a, b):
    return lax.dot_general(a, b, (((1,), (1,)), ((), ())), preferred_element_type=F32)


def step_kernel(
    kv_hbm,
    q_hbm,
    og_hbm,
    x_hbm,
    w_hbm,
    len_ref,
    fisher_out,
    merged_out,
    kv_ref,
    q_ref,
    og_ref,
    x_ref,
    w_ref,
    kv,
    score,
    slope,
    acc,
    p_ref,
    rs_in,
    xm,
    g,
    fb,
    ps,
    pr,
    ys,
    yr,
    mb,
    send_sems,
    recv_sems,
    block_send,
    block_recv,
    local_sems,
):
    at = Where()
    send = Sender(send_sems, recv_sems)
    x, z, y, core = at.x, at.z, at.y, at.core

    loads = []
    for n, (src, dst) in enumerate(
        ((kv_hbm, kv_ref), (q_hbm, q_ref), (og_hbm, og_ref), (x_hbm, x_ref), (w_hbm, w_ref))
    ):
        copy = pltpu.make_async_copy(src, dst, local_sems.at[n])
        copy.start()
        loads.append(copy)
    meet(
        [at.along_z(k) for k in (4, 3, 5, 2, 6, 1, 7)]
        + [at.along_y(k) for k in (2, 1, 3)]
        + [at.along_y(k, True) for k in (2, 1, 3)]
        + [at.along_x(1), at.along_x(-1), at.other_core()]
    )

    def rows(z, x):
        return pl.ds(pl.multiple_of(z * 128 + x * 32, 32), 32)

    def half(z, x, part):
        return pl.ds(pl.multiple_of(z * 128 + x * 32 + part * 16, 16), 16)

    def columns(h):
        return pl.ds(pl.multiple_of(h * PAIR, PAIR), PAIR)

    loads[0].wait()
    steps = (1, 7, 2, 6, 3, 5, 4)
    arrive = {}
    for k in (4, 3, 5, 2, 6, 1, 7):
        arrive[k] = send.start(
            kv_ref.at[:, columns((z + k) % 8)], kv.at[rows(z, x)], at.along_z(k)
        )
    own = pltpu.make_async_copy(kv_ref.at[:, columns(z)], kv.at[rows(z, x)], local_sems.at[5])
    own.start()
    own.wait()
    first, second = [], []

    def spread(z):
        block = kv.at[rows(z, x)]
        first.append((z, send.start(block, block, at.along_x(1)), send.start(block, block, at.along_x(-1))))

    spread(z)
    for k in steps:
        arrive[k].wait_recv()
        spread((z + 8 - k) % 8)
    for z_of, up, down in first:
        up.wait_recv()
        block = kv.at[half(z_of, (x + 3) % 4, 0)]
        second.append(send.start(block, block, at.along_x(1)))
        down.wait_recv()
        block = kv.at[half(z_of, (x + 1) % 4, 1)]
        second.append(send.start(block, block, at.along_x(-1)))
    for copy in loads[1:3]:
        copy.wait()
    for copy in second:
        copy.wait_recv()

    factor = HD**-0.5
    ends = bounds(len_ref)
    blocks = TOK // BLK

    def block_copy(j):
        by = (j - x + 4) % 4
        done = pl.ds(j * BLK, BLK)
        return pltpu.make_async_remote_copy(
            src_ref=p_ref.at[done],
            dst_ref=rs_in.at[by - 1],
            send_sem=block_send.at[j],
            recv_sem=block_recv.at[by - 1],
            device_id=(at.task, z * 4 + j),
            device_id_type=MESH,
        )

    for i in reversed(range(blocks)):
        queries = pl.ds(i * BLK, BLK)
        low = max(0, i - 2)
        token = i * BLK + lax.broadcasted_iota(jnp.int32, (1, BLK), 1)
        opening = jnp.zeros_like(token)
        for s in range(3):
            opening = jnp.where(token >= ends[s], ends[s], opening)
        for m in range(2):
            lanes = pl.ds(m * HD, HD)
            query = q_ref[queries, lanes]
            cot = og_ref[queries, lanes]
            highest = jnp.full((1, BLK), NEGATIVE, F32)
            for j in range(low, i + 1):
                key = kv[pl.ds(j * BLK, BLK), 0:HD]
                place = j * BLK + lax.broadcasted_iota(jnp.int32, (BLK, BLK), 0)
                allowed = place >= opening
                if j == i:
                    allowed = allowed & (place <= token)
                s = jnp.where(allowed, dot_nt(key, query) * factor, NEGATIVE)
                score[j - low] = s
                highest = jnp.maximum(highest, jnp.max(s, axis=0, keepdims=True))
            total = jnp.zeros((1, BLK), F32)
            weighed = jnp.zeros((1, BLK), F32)
            for j in range(low, i + 1):
                e = jnp.exp(score[j - low] - highest)
                score[j - low] = e
                d = dot_nt(kv[pl.ds(j * BLK, BLK), HD:PAIR], cot)
                slope[j - low] = d
                total = total + jnp.sum(e, axis=0, keepdims=True)
                weighed = weighed + jnp.sum(e * d, axis=0, keepdims=True)
            inverse = 1.0 / total
            offset = weighed * inverse
            for j in range(low, i + 1):
                p = score[j - low] * inverse
                ds = (p * (slope[j - low] - offset)).astype(BF16)
                to = pl.ds(j * BLK, BLK)
                dk = jnp.dot(ds, query, preferred_element_type=F32)
                dv = jnp.dot(p.astype(BF16), cot, preferred_element_type=F32)
                if m == 0 and i == min(blocks - 1, j + 2):
                    acc[to, 0:HD] = dk
                    acc[to, HD:PAIR] = dv
                else:
                    acc[to, 0:HD] += dk
                    acc[to, HD:PAIR] += dv
        done = pl.ds(i * BLK, BLK)
        p_ref[done, 0:HD] = (acc[done, 0:HD] * factor).astype(BF16)
        p_ref[done, HD:PAIR] = acc[done, HD:PAIR].astype(BF16)

        @pl.when(x != i)
        def _(i=i):
            block_copy(i).start()

    loads[3].wait()
    starts = [0] + ends[:3]
    for hf in range(2):
        o = 2 * BLK * hf
        turned = jnp.concatenate(
            [
                x_ref[o : o + CUT],
                x_ref[o + BLK : o + BLK + CUT],
                x_ref[o + CUT : o + BLK],
                x_ref[o + BLK + CUT : o + 2 * BLK],
            ],
            axis=0,
        ).T
        pos = lax.broadcasted_iota(jnp.int32, (1, 2 * BLK), 1)
        late = pos - 2 * CUT
        token = o + jnp.where(
            pos < 2 * CUT,
            pos + jnp.where(pos >= CUT, BLK - CUT, 0),
            late + CUT + jnp.where(late >= REST, BLK - REST, 0),
        )
        for n in range(3):
            s = hf + n
            inside = jnp.where((token >= starts[s]) & (token < ends[s]), 1.0, 0.0).astype(BF16)
            masked = turned * inside
            for rb in range(2):
                xm[rb, hf, n * HD : (n + 1) * HD, :] = masked[rb * HD : (rb + 1) * HD]
    loads[4].wait()

    def cut_rows(q):
        return (q // 2, pl.ds(pl.multiple_of(CUT * (q % 2), CUT), CUT))

    def rest_rows(q):
        return (q // 2, pl.ds(pl.multiple_of(2 * CUT + REST * (q % 2), 32), REST))

    summed = p_ref[pl.ds(pl.multiple_of(x * BLK, BLK), BLK), :].astype(F32)
    for by in range(3):
        pltpu.make_async_remote_copy(
            src_ref=p_ref.at[0:BLK],
            dst_ref=rs_in.at[by],
            send_sem=block_send.at[0],
            recv_sem=block_recv.at[by],
            device_id=at.along_x(1),
            device_id_type=MESH,
        ).wait_recv()
        summed = summed + rs_in[by].astype(F32)
    summed = summed.astype(BF16)
    hf, r = cut_rows(x)
    g[z, hf, r, :] = summed[:CUT]
    hf, r = rest_rows(x)
    g[z, hf, r, :] = summed[CUT:]

    def ring_piece(h, place, base, size, part):
        q = (x + place) % 4
        unit = size // 2
        length = size if part is None else unit
        skip = 0 if part is None else part * unit
        start = pl.multiple_of(base + size * (q % 2) + skip, 16)
        return g.at[h, q // 2, pl.ds(start, length)]

    class AroundX:
        def __init__(self, h, base, size):
            self.h, self.base, self.size = h, base, size
            own = ring_piece(h, 0, base, size, None)
            self.up = send.start(own, own, at.along_x(1))
            self.down = send.start(own, own, at.along_x(-1))

        def pass_on(self):
            self.up.wait_recv()
            piece = ring_piece(self.h, 3, self.base, self.size, 0)
            self.up2 = send.start(piece, piece, at.along_x(1))
            self.down.wait_recv()
            piece = ring_piece(self.h, 1, self.base, self.size, 1)
            self.down2 = send.start(piece, piece, at.along_x(-1))

        def end(self):
            self.up2.wait_recv()
            self.down2.wait_recv()

    def head(k):
        return (z + k + 8) % 8

    def send_rest(h, way):
        hf, r = rest_rows(x)
        piece = g.at[h, hf, r]
        return send.start(piece, piece, at.along_z(way))

    def send_cut(h, hf, way):
        piece = g.at[h, hf, 0 : 2 * CUT]
        return send.start(piece, piece, at.along_z(way))

    heads = [0, -1, 1, -2, 2, -3, 3, 4]
    outs = []

    def fisher_rows(slot, h, rb):
        a = jnp.dot(xm[rb, 0], g[h, 0], preferred_element_type=F32)
        b = jnp.dot(xm[rb, 1], g[h, 1], preferred_element_type=F32)
        g0, g3 = a[:HD], b[2 * HD :]
        g1, g2 = a[HD : 2 * HD] + b[:HD], a[2 * HD :] + b[HD : 2 * HD]
        f = g0 * g0 + g1 * g1 + g2 * g2 + g3 * g3
        fb[slot, pl.ds(pl.multiple_of(rb * HD, HD), HD), :] = f
        return f

    def weights(h, rb):
        return w_ref[pl.ds(pl.multiple_of(rb * HD, HD), HD), columns(h)].astype(F32)

    pair, over_y, merged_y, merged_core = {}, {}, {}, {}

    def compute_other(slot):
        h = head(heads[slot])
        rb = 1 - core
        f = fisher_rows(slot, h, rb)
        ps[slot, 0] = (f * weights(h, rb)).astype(BF16)
        ps[slot, 1] = f.astype(BF16)
        pair[slot] = send.start(ps.at[slot], pr.at[slot], at.other_core())

    def compute_own(slot):
        h = head(heads[slot])
        fisher_rows(slot, h, core)
        copy = pltpu.make_async_copy(fb.at[slot], fisher_out.at[:, columns(h)], local_sems.at[6 + slot])
        copy.start()
        outs.append(copy)

    def sum_pair(slot):
        h = head(heads[slot])
        pair[slot].wait_recv()
        f = fb[slot, pl.ds(pl.multiple_of(core * HD, HD), HD), :]
        ys[slot, 0] = (f * weights(h, core) + pr[slot, 0].astype(F32)).astype(BF16)
        ys[slot, 1] = (f + pr[slot, 1].astype(F32)).astype(BF16)
        over_y[slot] = []
        for k in (2, 1, 3):
            r = pl.ds(pl.multiple_of(((y + k) % 4) * 32, 32), 32)
            over_y[slot].append(send.start(ys.at[slot, :, r], yr.at[slot, k - 1], at.along_y(k)))

    def divide(slot):
        h = head(heads[slot])
        for copy in over_y[slot]:
            copy.wait_recv()
        r = pl.ds(pl.multiple_of(y * 32, 32), 32)
        sums = ys[slot, :, r, :].astype(F32)
        for k in range(3):
            sums = sums + yr[slot, k].astype(F32)
        to = pl.ds(pl.multiple_of(core * HD + y * 32, 32), 32)
        mb[h, to, :] = (sums[0] / (sums[1] + EPS)).astype(BF16)
        piece = mb.at[h, to]
        merged_y[slot] = [send.start(piece, piece, at.along_y(k)) for k in (2, 1, 3)]
        if slot == 7:
            merged_y[slot] += [send.start(piece, piece, at.along_y(k, True)) for k in (2, 1, 3)]
            merged_y[slot].append(send.start(piece, piece, at.other_core()))

    def share(slot):
        h = head(heads[slot])
        for copy in merged_y[slot]:
            copy.wait_recv()
        if slot < 7:
            piece = mb.at[h, pl.ds(pl.multiple_of(core * HD, HD), HD)]
            merged_core[slot] = send.start(piece, piece, at.other_core())

    def close(slot):
        h = head(heads[slot])
        if slot < 7:
            merged_core[slot].wait_recv()
        copy = pltpu.make_async_copy(mb.at[h], merged_out.at[:, columns(h)], local_sems.at[14 + slot])
        copy.start()
        outs.append(copy)

    stages = (sum_pair, divide, share, close)
    progress = {s: 0 for s in range(8)}

    def advance(upto):
        for slot in range(upto):
            if progress[slot] < len(stages):
                stages[progress[slot]](slot)
                progress[slot] += 1

    rings = {}
    rest = {"up": send_rest(z, 1), "down": send_rest(z, -1)}

    def rest_hop(k):
        if k < 4:
            rest["up"].wait_recv()
            if k < 3:
                rest["up"] = send_rest(head(-k), 1)
        rest["down"].wait_recv()
        if k < 4:
            rest["down"] = send_rest(head(k), -1)

    def around(slot):
        rings[slot] = AroundX(head(heads[slot]), 2 * CUT, REST)

    cut = {}

    def cut_hop(k, hf):
        last_up, last_down = (4, 3) if hf == 0 else (3, 4)
        if k <= last_up:
            cut["up", hf].wait_recv()
            if k < last_up:
                cut["up", hf] = send_cut(head(-k), hf, 1)
        if k <= last_down:
            cut["down", hf].wait_recv()
            if k < last_down:
                cut["down", hf] = send_cut(head(k), hf, -1)

    cut_ring = AroundX(z, 0, CUT)
    around(0)
    cut_ring.pass_on()
    rest_hop(1)
    around(1)
    cut_ring.end()
    for hf in range(2):
        for name, way in (("up", 1), ("down", -1)):
            cut[name, hf] = send_cut(z, hf, way)
    rings[0].pass_on()
    around(2)
    rest_hop(2)
    rings[0].end()
    compute_other(0)
    for j in range(1, 8):
        rings[j].pass_on()
        if j + 2 < 8:
            around(j + 2)
        if j == 1:
            compute_own(0)
        elif j == 2:
            rest_hop(3)
            cut_hop(1, 0)
        elif j == 3:
            cut_hop(1, 1)
            rings[1].end()
            compute_other(1)
            compute_own(1)
            rest_hop(4)
        elif j == 4:
            cut_hop(2, 0)
            rings[2].end()
            compute_other(2)
            compute_own(2)
        elif j == 5:
            cut_hop(2, 1)
            rings[3].end()
            compute_other(3)
            compute_own(3)
        elif j == 6:
            cut_hop(3, 0)
            rings[4].end()
            compute_other(4)
            compute_own(4)
        elif j == 7:
            cut_hop(3, 1)
            rings[5].end()
            compute_other(5)
            compute_own(5)
        advance(max(0, min(j - 2, 8)))
    rings[6].end()
    compute_other(6)
    compute_own(6)
    advance(6)
    cut_hop(4, 0)
    cut_hop(4, 1)
    rings[7].end()
    compute_other(7)
    compute_own(7)
    while any(progress[s] < len(stages) for s in range(8)):
        advance(8)
    send.finish()
    for copy in outs:
        copy.wait()
    for j in range(blocks):

        @pl.when(x != j)
        def _(j=j):
            block_copy(j).wait_send()


def write_kernel(fisher_ref, merged_ref, fisher_out, merged_out):
    fisher_out[...] = fisher_ref[...]
    merged_out[...] = merged_ref[...]


def body(layer_inputs, queries, key_values, out_grads, lengths, task_weights):
    hbm = pl.BlockSpec(memory_space=pl.ANY)
    wide = KVH * PAIR
    results = (
        jax.ShapeDtypeStruct((BLK, wide), F32),
        jax.ShapeDtypeStruct((BLK, wide), BF16),
    )
    fisher, merged = pl.pallas_call(
        step_kernel,
        out_shape=results,
        in_specs=[hbm] * 5 + [pl.BlockSpec(memory_space=pltpu.SMEM)],
        out_specs=(hbm, hbm),
        scratch_shapes=[
            pltpu.VMEM((TOK // 32, wide), BF16),
            pltpu.VMEM((TOK, PAIR), BF16),
            pltpu.VMEM((TOK, PAIR), BF16),
            pltpu.VMEM((TOK, BLK), BF16),
            pltpu.VMEM((BLK, wide), BF16),
            pltpu.VMEM((TOK, PAIR), BF16),
            pltpu.VMEM((3, BLK, BLK), F32),
            pltpu.VMEM((3, BLK, BLK), F32),
            pltpu.VMEM((TOK, PAIR), F32),
            pltpu.VMEM((TOK, PAIR), BF16),
            pltpu.VMEM((3, BLK, PAIR), BF16),
            pltpu.VMEM((2, 2, 3 * HD, 2 * BLK), BF16),
            pltpu.VMEM((KVH, 2, 2 * BLK, PAIR), BF16),
            pltpu.VMEM((8, BLK, PAIR), F32),
            pltpu.VMEM((8, 2, HD, PAIR), BF16),
            pltpu.VMEM((8, 2, HD, PAIR), BF16),
            pltpu.VMEM((8, 2, HD, PAIR), BF16),
            pltpu.VMEM((8, 3, 2, 32, PAIR), BF16),
            pltpu.VMEM((KVH, BLK, PAIR), BF16),
            pltpu.SemaphoreType.DMA((SEMS,)),
            pltpu.SemaphoreType.DMA((SEMS,)),
            pltpu.SemaphoreType.DMA((4,)),
            pltpu.SemaphoreType.DMA((3,)),
            pltpu.SemaphoreType.DMA((22,)),
        ],
        compiler_params=pltpu.CompilerParams(collective_id=0, has_side_effects=True),
        name="step",
    )(key_values[0], queries[0], out_grads[0], layer_inputs[0], task_weights[0], lengths)
    blocks = [
        pl.BlockSpec((BLK // 4, wide), lambda i: (i, 0)),
        pl.BlockSpec((BLK // 4, wide), lambda i: (i, 0)),
    ]
    fisher, merged = pl.pallas_call(
        write_kernel,
        out_shape=results,
        grid=(4,),
        in_specs=blocks,
        out_specs=tuple(blocks),
        name="write",
    )(fisher, merged)
    return fisher[None], merged


def solution(mesh):
    placed = (
        P("task", None, "col"),
        P("task", None, "col"),
        P("task", "col", None),
        P("task", None, "col"),
        P("task", None),
        P("task", "col", None),
    )
    return jax.shard_map(
        body,
        mesh=mesh,
        in_specs=placed,
        out_specs=(P("task", "col", None), P("col", None)),
        check_vma=False,
    )
```

time: 114 us -> 99.9 us (0.88)
  Pallas kernels: 109 us -> 99.1 us
  local copies, waits for them, and re-layouts: 4.2 us -> 0 us
    pallas_call x2, Pallas kernels: 109 us -> 99.1 us  [the longest x1 94.9 us: body(): pl.pallas_call(step_kernel, out_shape=results, in_specs=[hbm] * 5 + [pl.B...]
    unnamed x4 -> x0, local copies, waits for them, and re-layouts: 4.2 us -> none
where the time goes in v2:
time: 99.9 us; the launch traced here: 99.7 us
  Pallas kernels  99.1 us (99%)
    pallas_call x1, Pallas kernels, body(): pl.pallas_call(step_kernel, out_shape=results, in_specs=[hbm] * 5 + [pl.B...  94.9 us
    pallas_call x1, Pallas kernels, body(): pl.pallas_call(write_kernel, out_shape=results, grid=(4,), in_specs=block...  4.14 us

profile of v2, /device:TPU:1, one launch (start us, length us, event | category | flops | bytes accessed | tf_op | source)
XLA Modules:
  0.0 99.7 jit_solution(7975483262915947285)
XLA Ops:
  0.6 94.9 %step.1 = (f32[256,2048]{1,0:T(8,128)}, bf16[256,2048]{1,0:T(8,128)(2,1)}) custom-call(bf16[32,2048]{1,0:T(8,128)(2,1)} %bitcast.10, bf16[1024,256]{1,0:T(8,128)(2,1)} %bitcast.7, bf16[1024,256]{1,0:T(8,128)(2,1)} %bitcast.8, bf16[1024,256]{1,0:T(8,128)(2,1)} %bitcast.9, bf16[256,2048]{1,0:T(8,128)(2,1)} %bitcast.6, s32[1,4]{1,0:T(1,128)} %len_ref.1), custom_call_target="tpu_custom_call" | custom-call | tf_op jit(solution)/shard_map/step/pallas_call | solution.py:532
  95.6 4.1 %write.1 = (f32[256,2048]{1,0:T(8,128)}, bf16[256,2048]{1,0:T(8,128)(2,1)}) custom-call(f32[256,2048]{1,0:T(8,128)} %get-tuple-element.6.fisher_ref, bf16[256,2048]{1,0:T(8,128)(2,1)} %get-tuple-element.7.merged_ref), custom_call_target="tpu_custom_call" | custom-call | tf_op jit(solution)/shard_map/write/pallas_call | solution.py:570

commit v3 on v2

--- a/solution.py
+++ b/solution.py
@@ -18,7 +18,8 @@
 REST = BLK - CUT
 EPS = 1e-06
 NEGATIVE = -1e30
-SEMS = 164
+TURNS = 24
+SEMS = 88
 
 
 class Where:
@@ -50,15 +51,23 @@
 
 class Sender:
     def __init__(self, send_sems, recv_sems):
-        self.send_sems, self.recv_sems, self.copies = send_sems, recv_sems, []
-
-    def start(self, src, dst, device):
+        self.send_sems, self.recv_sems = send_sems, recv_sems
+        self.copies, self.used = [], 0
+
+    def fresh(self):
+        self.used += 1
+        assert self.used <= SEMS
+        return self.recv_sems.at[self.used - 1]
+
+    def start(self, src, dst, device, recv_sem=None):
         at = len(self.copies)
+        if at >= TURNS:
+            self.copies[at - TURNS].wait_send()
         copy = pltpu.make_async_remote_copy(
             src_ref=src,
             dst_ref=dst,
-            send_sem=self.send_sems.at[at],
-            recv_sem=self.recv_sems.at[at],
+            send_sem=self.send_sems.at[at % TURNS],
+            recv_sem=self.fresh() if recv_sem is None else recv_sem,
             device_id=device,
             device_id_type=MESH,
         )
@@ -66,8 +75,18 @@
         self.copies.append(copy)
         return copy
 
+    def arrived(self, ref, recv_sem):
+        pltpu.make_async_remote_copy(
+            src_ref=ref,
+            dst_ref=ref,
+            send_sem=self.send_sems.at[0],
+            recv_sem=recv_sem,
+            device_id=(0, 0),
+            device_id_type=MESH,
+        ).wait_recv()
+
     def finish(self):
-        for copy in self.copies:
+        for copy in self.copies[-TURNS:]:
             copy.wait_send()
 
 
@@ -132,48 +151,41 @@
         [at.along_z(k) for k in (4, 3, 5, 2, 6, 1, 7)]
         + [at.along_y(k) for k in (2, 1, 3)]
         + [at.along_y(k, True) for k in (2, 1, 3)]
-        + [at.along_x(1), at.along_x(-1), at.other_core()]
+        + [at.along_x(2), at.along_x(1), at.along_x(-1), at.other_core()]
     )
 
     def rows(z, x):
         return pl.ds(pl.multiple_of(z * 128 + x * 32, 32), 32)
 
-    def half(z, x, part):
-        return pl.ds(pl.multiple_of(z * 128 + x * 32 + part * 16, 16), 16)
-
     def columns(h):
         return pl.ds(pl.multiple_of(h * PAIR, PAIR), PAIR)
 
     loads[0].wait()
-    steps = (1, 7, 2, 6, 3, 5, 4)
-    arrive = {}
-    for k in (4, 3, 5, 2, 6, 1, 7):
-        arrive[k] = send.start(
-            kv_ref.at[:, columns((z + k) % 8)], kv.at[rows(z, x)], at.along_z(k)
-        )
     own = pltpu.make_async_copy(kv_ref.at[:, columns(z)], kv.at[rows(z, x)], local_sems.at[5])
     own.start()
+    steps = (1, 7, 2, 6, 3, 5, 4)
+    spare = {k: send.fresh() for k in steps}
+    arrive = {
+        k: send.start(kv_ref.at[:, columns((z + k) % 8)], kv.at[rows(z, x)], at.along_z(k), spare[k])
+        for k in steps
+    }
+    spare = list(spare.values())
+    spread = []
+
+    def spread_block(z):
+        block = kv.at[rows(z, x)]
+        for by in (2, 1, -1):
+            spare.append(send.fresh())
+            spread.append(send.start(block, block, at.along_x(by), spare[-1]))
+
     own.wait()
-    first, second = [], []
-
-    def spread(z):
-        block = kv.at[rows(z, x)]
-        first.append((z, send.start(block, block, at.along_x(1)), send.start(block, block, at.along_x(-1))))
-
-    spread(z)
+    spread_block(z)
     for k in steps:
         arrive[k].wait_recv()
-        spread((z + 8 - k) % 8)
-    for z_of, up, down in first:
-        up.wait_recv()
-        block = kv.at[half(z_of, (x + 3) % 4, 0)]
-        second.append(send.start(block, block, at.along_x(1)))
-        down.wait_recv()
-        block = kv.at[half(z_of, (x + 1) % 4, 1)]
-        second.append(send.start(block, block, at.along_x(-1)))
+        spread_block((z + 8 - k) % 8)
     for copy in loads[1:3]:
         copy.wait()
-    for copy in second:
+    for copy in spread:
         copy.wait_recv()
 
     factor = HD**-0.5
@@ -303,20 +315,23 @@
         start = pl.multiple_of(base + size * (q % 2) + skip, 16)
         return g.at[h, q // 2, pl.ds(start, length)]
 
+    def around_copy(piece, way):
+        return send.start(piece, piece, at.along_x(way), spare.pop(0) if spare else None)
+
     class AroundX:
         def __init__(self, h, base, size):
             self.h, self.base, self.size = h, base, size
             own = ring_piece(h, 0, base, size, None)
-            self.up = send.start(own, own, at.along_x(1))
-            self.down = send.start(own, own, at.along_x(-1))
+            self.up = around_copy(own, 1)
+            self.down = around_copy(own, -1)
 
         def pass_on(self):
             self.up.wait_recv()
             piece = ring_piece(self.h, 3, self.base, self.size, 0)
-            self.up2 = send.start(piece, piece, at.along_x(1))
+            self.up2 = around_copy(piece, 1)
             self.down.wait_recv()
             piece = ring_piece(self.h, 1, self.base, self.size, 1)
-            self.down2 = send.start(piece, piece, at.along_x(-1))
+            self.down2 = around_copy(piece, -1)
 
         def end(self):
             self.up2.wait_recv()
@@ -335,7 +350,6 @@
         return send.start(piece, piece, at.along_z(way))
 
     heads = [0, -1, 1, -2, 2, -3, 3, 4]
-    outs = []
 
     def fisher_rows(slot, h, rb):
         a = jnp.dot(xm[rb, 0], g[h, 0], preferred_element_type=F32)
@@ -362,9 +376,7 @@
     def compute_own(slot):
         h = head(heads[slot])
         fisher_rows(slot, h, core)
-        copy = pltpu.make_async_copy(fb.at[slot], fisher_out.at[:, columns(h)], local_sems.at[6 + slot])
-        copy.start()
-        outs.append(copy)
+        pltpu.make_async_copy(fb.at[slot], fisher_out.at[:, columns(h)], local_sems.at[6]).start()
 
     def sum_pair(slot):
         h = head(heads[slot])
@@ -372,15 +384,14 @@
         f = fb[slot, pl.ds(pl.multiple_of(core * HD, HD), HD), :]
         ys[slot, 0] = (f * weights(h, core) + pr[slot, 0].astype(F32)).astype(BF16)
         ys[slot, 1] = (f + pr[slot, 1].astype(F32)).astype(BF16)
-        over_y[slot] = []
+        over_y[slot] = send.fresh()
         for k in (2, 1, 3):
             r = pl.ds(pl.multiple_of(((y + k) % 4) * 32, 32), 32)
-            over_y[slot].append(send.start(ys.at[slot, :, r], yr.at[slot, k - 1], at.along_y(k)))
+            send.start(ys.at[slot, :, r], yr.at[slot, k - 1], at.along_y(k), over_y[slot])
 
     def divide(slot):
         h = head(heads[slot])
-        for copy in over_y[slot]:
-            copy.wait_recv()
+        send.arrived(yr.at[slot], over_y[slot])
         r = pl.ds(pl.multiple_of(y * 32, 32), 32)
         sums = ys[slot, :, r, :].astype(F32)
         for k in range(3):
@@ -388,15 +399,17 @@
         to = pl.ds(pl.multiple_of(core * HD + y * 32, 32), 32)
         mb[h, to, :] = (sums[0] / (sums[1] + EPS)).astype(BF16)
         piece = mb.at[h, to]
-        merged_y[slot] = [send.start(piece, piece, at.along_y(k)) for k in (2, 1, 3)]
+        merged_y[slot] = send.fresh()
+        for k in (2, 1, 3):
+            send.start(piece, piece, at.along_y(k), merged_y[slot])
         if slot == 7:
-            merged_y[slot] += [send.start(piece, piece, at.along_y(k, True)) for k in (2, 1, 3)]
-            merged_y[slot].append(send.start(piece, piece, at.other_core()))
+            for k in (2, 1, 3):
+                send.start(piece, piece, at.along_y(k, True), merged_y[slot])
+            send.start(piece, piece, at.other_core(), merged_y[slot])
 
     def share(slot):
         h = head(heads[slot])
-        for copy in merged_y[slot]:
-            copy.wait_recv()
+        send.arrived(mb.at[h, 0 : 224 if slot == 7 else 96], merged_y[slot])
         if slot < 7:
             piece = mb.at[h, pl.ds(pl.multiple_of(core * HD, HD), HD)]
             merged_core[slot] = send.start(piece, piece, at.other_core())
@@ -405,18 +418,7 @@
         h = head(heads[slot])
         if slot < 7:
             merged_core[slot].wait_recv()
-        copy = pltpu.make_async_copy(mb.at[h], merged_out.at[:, columns(h)], local_sems.at[14 + slot])
-        copy.start()
-        outs.append(copy)
-
-    stages = (sum_pair, divide, share, close)
-    progress = {s: 0 for s in range(8)}
-
-    def advance(upto):
-        for slot in range(upto):
-            if progress[slot] < len(stages):
-                stages[progress[slot]](slot)
-                progress[slot] += 1
+        pltpu.make_async_copy(mb.at[h], merged_out.at[:, columns(h)], local_sems.at[7]).start()
 
     rings = {}
     rest = {"up": send_rest(z, 1), "down": send_rest(z, -1)}
@@ -446,70 +448,73 @@
             if k < last_down:
                 cut["down", hf] = send_cut(head(k), hf, -1)
 
+    def further(slot):
+        rings[slot].pass_on()
+        if slot + 2 < 8:
+            around(slot + 2)
+
     cut_ring = AroundX(z, 0, CUT)
+    cut_ring.pass_on()
     around(0)
-    cut_ring.pass_on()
     rest_hop(1)
     around(1)
     cut_ring.end()
     for hf in range(2):
         for name, way in (("up", 1), ("down", -1)):
             cut[name, hf] = send_cut(z, hf, way)
-    rings[0].pass_on()
-    around(2)
+    further(0)
     rest_hop(2)
+    further(1)
     rings[0].end()
     compute_other(0)
-    for j in range(1, 8):
-        rings[j].pass_on()
-        if j + 2 < 8:
-            around(j + 2)
-        if j == 1:
-            compute_own(0)
-        elif j == 2:
-            rest_hop(3)
-            cut_hop(1, 0)
-        elif j == 3:
-            cut_hop(1, 1)
-            rings[1].end()
-            compute_other(1)
-            compute_own(1)
-            rest_hop(4)
-        elif j == 4:
-            cut_hop(2, 0)
-            rings[2].end()
-            compute_other(2)
-            compute_own(2)
-        elif j == 5:
-            cut_hop(2, 1)
-            rings[3].end()
-            compute_other(3)
-            compute_own(3)
-        elif j == 6:
-            cut_hop(3, 0)
-            rings[4].end()
-            compute_other(4)
-            compute_own(4)
-        elif j == 7:
-            cut_hop(3, 1)
-            rings[5].end()
-            compute_other(5)
-            compute_own(5)
-        advance(max(0, min(j - 2, 8)))
-    rings[6].end()
-    compute_other(6)
-    compute_own(6)
-    advance(6)
-    cut_hop(4, 0)
+    compute_own(0)
+    sum_pair(0)
+    cut_hop(1, 0)
+    for k in range(1, 4):
+        a, b = 2 * k - 1, 2 * k
+        further(b)
+        if k < 3:
+            rest_hop(k + 2)
+        cut_hop(k, 1)
+        rings[a].end()
+        compute_other(a)
+        compute_own(a)
+        further(b + 1)
+        for slot in (a - 2, b - 2):
+            if slot >= 0:
+                divide(slot)
+        rings[b].end()
+        compute_other(b)
+        sum_pair(a)
+        compute_own(b)
+        sum_pair(b)
+        for slot in (a - 4, b - 4):
+            if slot >= 0:
+                share(slot)
+        cut_hop(k + 1, 0)
     cut_hop(4, 1)
     rings[7].end()
     compute_other(7)
     compute_own(7)
-    while any(progress[s] < len(stages) for s in range(8)):
-        advance(8)
+    sum_pair(7)
+    close(0)
+    for slot in (5, 6):
+        divide(slot)
+    for slot in (3, 4):
+        share(slot)
+    divide(7)
+    for slot in (1, 2):
+        close(slot)
+    for slot in (5, 6):
+        share(slot)
+    for slot in (3, 4):
+        close(slot)
+    share(7)
+    for slot in (7, 5, 6):
+        close(slot)
     send.finish()
-    for copy in outs:
-        copy.wait()
+    pltpu.make_async_copy(fb, fb, local_sems.at[6]).wait()
+    pltpu.make_async_copy(mb, mb, local_sems.at[7]).wait()
     for j in range(blocks):
 
         @pl.when(x != j)
@@ -517,9 +522,26 @@
             block_copy(j).wait_send()
 
 
-def write_kernel(fisher_ref, merged_ref, fisher_out, merged_out):
-    fisher_out[...] = fisher_ref[...]
-    merged_out[...] = merged_ref[...]
+def write_kernel(fisher_ref, merged_ref, fisher_out, merged_out, fisher, merged, in_sems, out_sems):
+    copies = []
+    for n in range(8):
+        src, held, dst = (
+            (fisher_ref, fisher, fisher_out) if n < 4 else (merged_ref, merged, merged_out)
+        )
+        r = pl.ds((n % 4) * (BLK // 4), BLK // 4)
+        copies.append(
+            (
+                pltpu.make_async_copy(src.at[r], held.at[r], in_sems.at[n]),
+                pltpu.make_async_copy(held.at[r], dst.at[r], out_sems.at[n]),
+            )
+        )
+    for come, go in copies:
+        come.start()
+    for come, go in copies:
+        come.wait()
+        go.start()
+    for come, go in copies:
+        go.wait()
 
 
 def body(layer_inputs, queries, key_values, out_grads, lengths, task_weights):
@@ -554,25 +576,26 @@
             pltpu.VMEM((8, 2, HD, PAIR), BF16),
             pltpu.VMEM((8, 3, 2, 32, PAIR), BF16),
             pltpu.VMEM((KVH, BLK, PAIR), BF16),
-            pltpu.SemaphoreType.DMA((SEMS,)),
+            pltpu.SemaphoreType.DMA((TURNS,)),
             pltpu.SemaphoreType.DMA((SEMS,)),
             pltpu.SemaphoreType.DMA((4,)),
             pltpu.SemaphoreType.DMA((3,)),
-            pltpu.SemaphoreType.DMA((22,)),
+            pltpu.SemaphoreType.DMA((8,)),
         ],
         compiler_params=pltpu.CompilerParams(collective_id=0, has_side_effects=True),
         name="step",
     )(key_values[0], queries[0], out_grads[0], layer_inputs[0], task_weights[0], lengths)
-    blocks = [
-        pl.BlockSpec((BLK // 4, wide), lambda i: (i, 0)),
-        pl.BlockSpec((BLK // 4, wide), lambda i: (i, 0)),
-    ]
     fisher, merged = pl.pallas_call(
         write_kernel,
         out_shape=results,
-        grid=(4,),
-        in_specs=blocks,
-        out_specs=tuple(blocks),
+        in_specs=[hbm, hbm],
+        out_specs=(hbm, hbm),
+        scratch_shapes=[
+            pltpu.VMEM((BLK, wide), F32),
+            pltpu.VMEM((BLK, wide), BF16),
+            pltpu.SemaphoreType.DMA((8,)),
+            pltpu.SemaphoreType.DMA((8,)),
+        ],
         name="write",
     )(fisher, merged)
     return fisher[None], merged

time: 99.9 us -> 79.7 us (0.80)
  Pallas kernels: 99.1 us -> 79 us
    pallas_call x1, Pallas kernels: 94.9 us -> 76.1 us  [body(): pl.pallas_call(step_kernel, out_shape=results, in_specs=[hbm] * 5 + [pl.B...]
    pallas_call x1, Pallas kernels: 4.14 us -> 2.83 us  [body(): pl.pallas_call(write_kernel, out_shape=results, in_specs=[hbm, hbm], out_...]
where the time goes in v3:
time: 79.7 us; the launch traced here: 79.6 us
  Pallas kernels  79 us (99%)
    pallas_call x1, Pallas kernels, body(): pl.pallas_call(step_kernel, out_shape=results, in_specs=[hbm] * 5 + [pl.B...  76.1 us
    pallas_call x1, Pallas kernels, body(): pl.pallas_call(write_kernel, out_shape=results, in_specs=[hbm, hbm], out_...  2.83 us

profile of v3, /device:TPU:1, one launch (start us, length us, event | category | flops | bytes accessed | tf_op | source)
XLA Modules:
  0.0 79.6 jit_solution(5537671194998753260)
XLA Ops:
  0.6 76.1 %step.1 = (f32[256,2048]{1,0:T(8,128)}, bf16[256,2048]{1,0:T(8,128)(2,1)}) custom-call(bf16[32,2048]{1,0:T(8,128)(2,1)} %bitcast.10, bf16[1024,256]{1,0:T(8,128)(2,1)} %bitcast.7, bf16[1024,256]{1,0:T(8,128)(2,1)} %bitcast.8, bf16[1024,256]{1,0:T(8,128)(2,1)} %bitcast.9, bf16[256,2048]{1,0:T(8,128)(2,1)} %bitcast.6, s32[1,4]{1,0:T(1,128)} %len_ref.1), custom_call_target="tpu_custom_call" | custom-call | tf_op jit(solution)/shard_map/step/pallas_call | solution.py:554
  76.8 2.8 %write.1 = (f32[256,2048]{1,0:T(8,128)}, bf16[256,2048]{1,0:T(8,128)(2,1)}) custom-call(f32[256,2048]{1,0:T(8,128)} %get-tuple-element.6.fisher_ref, bf16[256,2048]{1,0:T(8,128)(2,1)} %get-tuple-element.7.merged_ref), custom_call_target="tpu_custom_call" | custom-call | tf_op jit(solution)/shard_map/write/pallas_call | solution.py:588

commit v4 on v3

--- a/solution.py
+++ b/solution.py
@@ -14,12 +14,13 @@
 PAIR = 2 * HD
 TOK = 1024
 BLK = 256
-CUT = 96
-REST = BLK - CUT
+OWN = BLK // 4
+CUT = 48
+REST = 2 * OWN - CUT
 EPS = 1e-06
 NEGATIVE = -1e30
 TURNS = 24
-SEMS = 88
+SEMS = 96
 
 
 class Where:
@@ -132,8 +133,6 @@
     mb,
     send_sems,
     recv_sems,
-    block_send,
-    block_recv,
     local_sems,
 ):
     at = Where()
@@ -192,17 +191,14 @@
     ends = bounds(len_ref)
     blocks = TOK // BLK
 
-    def block_copy(j):
-        by = (j - x + 4) % 4
-        done = pl.ds(j * BLK, BLK)
-        return pltpu.make_async_remote_copy(
-            src_ref=p_ref.at[done],
-            dst_ref=rs_in.at[by - 1],
-            send_sem=block_send.at[j],
-            recv_sem=block_recv.at[by - 1],
-            device_id=(at.task, z * 4 + j),
-            device_id_type=MESH,
-        )
+    def piece_of(j, by):
+        return pl.ds(pl.multiple_of(j * BLK + ((x + by + 4) % 4) * OWN, OWN), OWN)
+
+    block_sems = [send.fresh() for j in range(blocks)]
+
+    def send_block(j):
+        for by in (2, 1, 3):
+            send.start(p_ref.at[piece_of(j, by)], rs_in.at[j, by - 1], at.along_x(by), block_sems[j])
 
     for i in reversed(range(blocks)):
         queries = pl.ds(i * BLK, BLK)
@@ -251,31 +247,28 @@
         done = pl.ds(i * BLK, BLK)
         p_ref[done, 0:HD] = (acc[done, 0:HD] * factor).astype(BF16)
         p_ref[done, HD:PAIR] = acc[done, HD:PAIR].astype(BF16)
-
-        @pl.when(x != i)
-        def _(i=i):
-            block_copy(i).start()
+        send_block(i)
 
     loads[3].wait()
     starts = [0] + ends[:3]
     for hf in range(2):
         o = 2 * BLK * hf
-        turned = jnp.concatenate(
-            [
-                x_ref[o : o + CUT],
-                x_ref[o + BLK : o + BLK + CUT],
-                x_ref[o + CUT : o + BLK],
-                x_ref[o + BLK + CUT : o + 2 * BLK],
-            ],
-            axis=0,
-        ).T
+        early = [x_ref[o + OWN * q : o + OWN * q + CUT] for q in range(4)]
+        late = []
+        for q in range(4):
+            late.append(x_ref[o + OWN * q + CUT : o + OWN * q + OWN])
+            late.append(x_ref[o + BLK + OWN * q : o + BLK + OWN * q + OWN])
+        turned = jnp.concatenate(early + late, axis=0).T
         pos = lax.broadcasted_iota(jnp.int32, (1, 2 * BLK), 1)
-        late = pos - 2 * CUT
-        token = o + jnp.where(
-            pos < 2 * CUT,
-            pos + jnp.where(pos >= CUT, BLK - CUT, 0),
-            late + CUT + jnp.where(late >= REST, BLK - REST, 0),
-        )
+        token = jnp.zeros_like(pos)
+        for q in range(4):
+            token = jnp.where(pos >= CUT * q, pos - CUT * q + OWN * q, token)
+        for q in range(4):
+            base = 4 * CUT + REST * q
+            token = jnp.where(pos >= base, pos - base + CUT + OWN * q, token)
+            base += OWN - CUT
+            token = jnp.where(pos >= base, pos - base + BLK + OWN * q, token)
+        token = token + o
         for n in range(3):
             s = hf + n
             inside = jnp.where((token >= starts[s]) & (token < ends[s]), 1.0, 0.0).astype(BF16)
@@ -285,53 +278,38 @@
     loads[4].wait()
 
     def cut_rows(q):
-        return (q // 2, pl.ds(pl.multiple_of(CUT * (q % 2), CUT), CUT))
-
-    def rest_rows(q):
-        return (q // 2, pl.ds(pl.multiple_of(2 * CUT + REST * (q % 2), 32), REST))
-
-    summed = p_ref[pl.ds(pl.multiple_of(x * BLK, BLK), BLK), :].astype(F32)
-    for by in range(3):
-        pltpu.make_async_remote_copy(
-            src_ref=p_ref.at[0:BLK],
-            dst_ref=rs_in.at[by],
-            send_sem=block_send.at[0],
-            recv_sem=block_recv.at[by],
-            device_id=at.along_x(1),
-            device_id_type=MESH,
-        ).wait_recv()
-        summed = summed + rs_in[by].astype(F32)
-    summed = summed.astype(BF16)
-    hf, r = cut_rows(x)
-    g[z, hf, r, :] = summed[:CUT]
-    hf, r = rest_rows(x)
-    g[z, hf, r, :] = summed[CUT:]
-
-    def ring_piece(h, place, base, size, part):
-        q = (x + place) % 4
-        unit = size // 2
-        length = size if part is None else unit
-        skip = 0 if part is None else part * unit
-        start = pl.multiple_of(base + size * (q % 2) + skip, 16)
-        return g.at[h, q // 2, pl.ds(start, length)]
+        return pl.ds(pl.multiple_of(CUT * (q % 4), CUT), CUT)
+
+    def rest_rows(q, skip=0, length=REST):
+        return pl.ds(pl.multiple_of(4 * CUT + REST * (q % 4) + skip, 16), length)
+
+    def settle(j):
+        send.arrived(rs_in.at[j], block_sems[j])
+        summed = p_ref[piece_of(j, 0), :].astype(F32)
+        for by in range(3):
+            summed = summed + rs_in[j, by].astype(F32)
+        summed = summed.astype(BF16)
+        if j % 2 == 0:
+            g[z, j // 2, cut_rows(x), :] = summed[:CUT]
+            g[z, j // 2, rest_rows(x, 0, OWN - CUT), :] = summed[CUT:]
+        else:
+            g[z, j // 2, rest_rows(x, OWN - CUT, OWN), :] = summed
 
     def around_copy(piece, way):
         return send.start(piece, piece, at.along_x(way), spare.pop(0) if spare else None)
 
-    class AroundX:
-        def __init__(self, h, base, size):
-            self.h, self.base, self.size = h, base, size
-            own = ring_piece(h, 0, base, size, None)
+    class Ring:
+        def __init__(self, h):
+            self.h = h
+            own = g.at[h, :, rest_rows(x)]
             self.up = around_copy(own, 1)
             self.down = around_copy(own, -1)
 
         def pass_on(self):
             self.up.wait_recv()
-            piece = ring_piece(self.h, 3, self.base, self.size, 0)
-            self.up2 = around_copy(piece, 1)
+            self.up2 = around_copy(g.at[self.h, 0, rest_rows(x + 3)], 1)
             self.down.wait_recv()
-            piece = ring_piece(self.h, 1, self.base, self.size, 1)
-            self.down2 = around_copy(piece, -1)
+            self.down2 = around_copy(g.at[self.h, 1, rest_rows(x + 1)], -1)
 
         def end(self):
             self.up2.wait_recv()
@@ -341,12 +319,11 @@
         return (z + k + 8) % 8
 
     def send_rest(h, way):
-        hf, r = rest_rows(x)
-        piece = g.at[h, hf, r]
+        piece = g.at[h, :, rest_rows(x)]
         return send.start(piece, piece, at.along_z(way))
 
     def send_cut(h, hf, way):
-        piece = g.at[h, hf, 0 : 2 * CUT]
+        piece = g.at[h, hf, 0 : 4 * CUT]
         return send.start(piece, piece, at.along_z(way))
 
     heads = [0, -1, 1, -2, 2, -3, 3, 4]
@@ -421,19 +398,27 @@
         pltpu.make_async_copy(mb.at[h], merged_out.at[:, columns(h)], local_sems.at[7]).start()
 
     rings = {}
-    rest = {"up": send_rest(z, 1), "down": send_rest(z, -1)}
+    rest = {}
+    rest_first = {"up": send.fresh(), "down": send.fresh()}
+    ways = (("up", 1), ("down", -1))
+
+    def rest_arrives(name, k):
+        if k == 1:
+            send.arrived(g.at[z, :, rest_rows(x)], rest_first[name])
+        else:
+            rest[name].wait_recv()
 
     def rest_hop(k):
         if k < 4:
-            rest["up"].wait_recv()
+            rest_arrives("up", k)
             if k < 3:
                 rest["up"] = send_rest(head(-k), 1)
-        rest["down"].wait_recv()
+        rest_arrives("down", k)
         if k < 4:
             rest["down"] = send_rest(head(k), -1)
 
     def around(slot):
-        rings[slot] = AroundX(head(heads[slot]), 2 * CUT, REST)
+        rings[slot] = Ring(head(heads[slot]))
 
     cut = {}
 
@@ -453,73 +438,66 @@
         if slot + 2 < 8:
             around(slot + 2)
 
-    cut_ring = AroundX(z, 0, CUT)
-    cut_ring.pass_on()
+    cut_ring = {}
+    for hf in (1, 0):
+        settle(2 * hf + 1)
+        settle(2 * hf)
+        for name, way in ways:
+            piece = g.at[z, hf, cut_rows(x)]
+            cut_ring[name, hf] = around_copy(piece, way)
+        for name, way in ways:
+            piece = g.at[z, hf, rest_rows(x)]
+            send.start(piece, piece, at.along_z(way), rest_first[name])
+    cut_ring["up", 1].wait_recv()
+    far_up = around_copy(g.at[z, 1, cut_rows(x + 3)], 1)
+    cut_ring["down", 0].wait_recv()
+    far_down = around_copy(g.at[z, 0, cut_rows(x + 1)], -1)
     around(0)
     rest_hop(1)
     around(1)
-    cut_ring.end()
-    for hf in range(2):
-        for name, way in (("up", 1), ("down", -1)):
-            cut[name, hf] = send_cut(z, hf, way)
+    cut_ring["down", 1].wait_recv()
+    far_up.wait_recv()
+    for name, way in ways:
+        cut[name, 1] = send_cut(z, 1, way)
+    cut_ring["up", 0].wait_recv()
+    far_down.wait_recv()
+    for name, way in ways:
+        cut[name, 0] = send_cut(z, 0, way)
     further(0)
     rest_hop(2)
     further(1)
-    rings[0].end()
-    compute_other(0)
-    compute_own(0)
-    sum_pair(0)
-    cut_hop(1, 0)
-    for k in range(1, 4):
-        a, b = 2 * k - 1, 2 * k
-        further(b)
-        if k < 3:
-            rest_hop(k + 2)
-        cut_hop(k, 1)
-        rings[a].end()
-        compute_other(a)
-        compute_own(a)
-        further(b + 1)
-        for slot in (a - 2, b - 2):
-            if slot >= 0:
-                divide(slot)
-        rings[b].end()
-        compute_other(b)
-        sum_pair(a)
-        compute_own(b)
-        sum_pair(b)
-        for slot in (a - 4, b - 4):
-            if slot >= 0:
-                share(slot)
-        cut_hop(k + 1, 0)
-    cut_hop(4, 1)
-    rings[7].end()
-    compute_other(7)
-    compute_own(7)
-    sum_pair(7)
+    for slot in range(8):
+        rings[slot].end()
+        compute_other(slot)
+        compute_own(slot)
+        if slot + 2 < 8:
+            further(slot + 2)
+        if slot in (0, 2):
+            rest_hop(slot // 2 + 3)
+        if slot % 2 == 0 and slot < 7:
+            cut_hop(slot // 2 + 1, 1)
+            cut_hop(slot // 2 + 1, 0)
+        sum_pair(slot)
+        if slot >= 2:
+            divide(slot - 2)
+        if slot >= 4:
+            share(slot - 4)
+    divide(6)
+    share(4)
     close(0)
-    for slot in (5, 6):
-        divide(slot)
-    for slot in (3, 4):
-        share(slot)
+    close(1)
     divide(7)
-    for slot in (1, 2):
-        close(slot)
-    for slot in (5, 6):
-        share(slot)
-    for slot in (3, 4):
-        close(slot)
+    close(2)
+    share(5)
+    close(3)
+    close(4)
+    share(6)
     share(7)
     for slot in (7, 5, 6):
         close(slot)
     send.finish()
     pltpu.make_async_copy(fb, fb, local_sems.at[6]).wait()
     pltpu.make_async_copy(mb, mb, local_sems.at[7]).wait()
-    for j in range(blocks):
-
-        @pl.when(x != j)
-        def _(j=j):
-            block_copy(j).wait_send()
 
 
 def write_kernel(fisher_ref, merged_ref, fisher_out, merged_out, fisher, merged, in_sems, out_sems):
@@ -567,7 +545,7 @@
             pltpu.VMEM((3, BLK, BLK), F32),
             pltpu.VMEM((TOK, PAIR), F32),
             pltpu.VMEM((TOK, PAIR), BF16),
-            pltpu.VMEM((3, BLK, PAIR), BF16),
+            pltpu.VMEM((4, 3, OWN, PAIR), BF16),
             pltpu.VMEM((2, 2, 3 * HD, 2 * BLK), BF16),
             pltpu.VMEM((KVH, 2, 2 * BLK, PAIR), BF16),
             pltpu.VMEM((8, BLK, PAIR), F32),
@@ -578,8 +556,6 @@
             pltpu.VMEM((KVH, BLK, PAIR), BF16),
             pltpu.SemaphoreType.DMA((TURNS,)),
             pltpu.SemaphoreType.DMA((SEMS,)),
-            pltpu.SemaphoreType.DMA((4,)),
-            pltpu.SemaphoreType.DMA((3,)),
             pltpu.SemaphoreType.DMA((8,)),
         ],
         compiler_params=pltpu.CompilerParams(collective_id=0, has_side_effects=True),

time: 79.7 us -> 74.5 us (0.935)
  Pallas kernels: 79 us -> 73.8 us
    pallas_call x1, Pallas kernels: 76.1 us -> 71 us  [body(): pl.pallas_call(step_kernel, out_shape=results, in_specs=[hbm] * 5 + [pl.B...]
where the time goes in v4:
time: 74.5 us; the launch traced here: 74.4 us
  Pallas kernels  73.8 us (99%)
    pallas_call x1, Pallas kernels, body(): pl.pallas_call(step_kernel, out_shape=results, in_specs=[hbm] * 5 + [pl.B...  71 us
    pallas_call x1, Pallas kernels, body(): pl.pallas_call(write_kernel, out_shape=results, in_specs=[hbm, hbm], out_...  2.83 us

profile of v4, /device:TPU:1, one launch (start us, length us, event | category | flops | bytes accessed | tf_op | source)
XLA Modules:
  0.0 74.4 jit_solution(7898784769342216519)
XLA Ops:
  0.6 71.0 %step.1 = (f32[256,2048]{1,0:T(8,128)}, bf16[256,2048]{1,0:T(8,128)(2,1)}) custom-call(bf16[32,2048]{1,0:T(8,128)(2,1)} %bitcast.10, bf16[1024,256]{1,0:T(8,128)(2,1)} %bitcast.7, bf16[1024,256]{1,0:T(8,128)(2,1)} %bitcast.8, bf16[1024,256]{1,0:T(8,128)(2,1)} %bitcast.9, bf16[256,2048]{1,0:T(8,128)(2,1)} %bitcast.6, s32[1,4]{1,0:T(1,128)} %len_ref.1), custom_call_target="tpu_custom_call" | custom-call | tf_op jit(solution)/shard_map/step/pallas_call | solution.py:532
  71.6 2.8 %write.1 = (f32[256,2048]{1,0:T(8,128)}, bf16[256,2048]{1,0:T(8,128)(2,1)}) custom-call(f32[256,2048]{1,0:T(8,128)} %get-tuple-element.6.fisher_ref, bf16[256,2048]{1,0:T(8,128)(2,1)} %get-tuple-element.7.merged_ref), custom_call_target="tpu_custom_call" | custom-call | tf_op jit(solution)/shard_map/write/pallas_call | solution.py:564

commit v5 on v4

--- a/solution.py
+++ b/solution.py
@@ -207,43 +207,49 @@
         opening = jnp.zeros_like(token)
         for s in range(3):
             opening = jnp.where(token >= ends[s], ends[s], opening)
-        for m in range(2):
-            lanes = pl.ds(m * HD, HD)
-            query = q_ref[queries, lanes]
-            cot = og_ref[queries, lanes]
-            highest = jnp.full((1, BLK), NEGATIVE, F32)
-            for j in range(low, i + 1):
-                key = kv[pl.ds(j * BLK, BLK), 0:HD]
-                place = j * BLK + lax.broadcasted_iota(jnp.int32, (BLK, BLK), 0)
-                allowed = place >= opening
-                if j == i:
-                    allowed = allowed & (place <= token)
-                s = jnp.where(allowed, dot_nt(key, query) * factor, NEGATIVE)
-                score[j - low] = s
-                highest = jnp.maximum(highest, jnp.max(s, axis=0, keepdims=True))
-            total = jnp.zeros((1, BLK), F32)
-            weighed = jnp.zeros((1, BLK), F32)
-            for j in range(low, i + 1):
-                e = jnp.exp(score[j - low] - highest)
-                score[j - low] = e
-                d = dot_nt(kv[pl.ds(j * BLK, BLK), HD:PAIR], cot)
-                slope[j - low] = d
-                total = total + jnp.sum(e, axis=0, keepdims=True)
-                weighed = weighed + jnp.sum(e * d, axis=0, keepdims=True)
-            inverse = 1.0 / total
-            offset = weighed * inverse
-            for j in range(low, i + 1):
-                p = score[j - low] * inverse
-                ds = (p * (slope[j - low] - offset)).astype(BF16)
-                to = pl.ds(j * BLK, BLK)
-                dk = jnp.dot(ds, query, preferred_element_type=F32)
-                dv = jnp.dot(p.astype(BF16), cot, preferred_element_type=F32)
-                if m == 0 and i == min(blocks - 1, j + 2):
-                    acc[to, 0:HD] = dk
-                    acc[to, HD:PAIR] = dv
-                else:
-                    acc[to, 0:HD] += dk
-                    acc[to, HD:PAIR] += dv
+        heads_in = [
+            (q_ref[queries, m * HD : m * HD + HD], og_ref[queries, m * HD : m * HD + HD])
+            for m in range(2)
+        ]
+        highest = [jnp.full((1, BLK), NEGATIVE, F32)] * 2
+        for j in range(low, i + 1):
+            key = kv[pl.ds(j * BLK, BLK), 0:HD]
+            place = j * BLK + lax.broadcasted_iota(jnp.int32, (BLK, BLK), 0)
+            allowed = place >= opening
+            if j == i:
+                allowed = allowed & (place <= token)
+            for m in range(2):
+                s = jnp.where(allowed, dot_nt(key, heads_in[m][0]) * factor, NEGATIVE)
+                score[m, j - low] = s
+                highest[m] = jnp.maximum(highest[m], jnp.max(s, axis=0, keepdims=True))
+        total = [jnp.zeros((1, BLK), F32)] * 2
+        weighed = [jnp.zeros((1, BLK), F32)] * 2
+        for j in range(low, i + 1):
+            value = kv[pl.ds(j * BLK, BLK), HD:PAIR]
+            for m in range(2):
+                e = jnp.exp(score[m, j - low] - highest[m])
+                score[m, j - low] = e
+                d = dot_nt(value, heads_in[m][1])
+                slope[m, j - low] = d
+                total[m] = total[m] + jnp.sum(e, axis=0, keepdims=True)
+                weighed[m] = weighed[m] + jnp.sum(e * d, axis=0, keepdims=True)
+        inverse = [1.0 / total[m] for m in range(2)]
+        offset = [weighed[m] * inverse[m] for m in range(2)]
+        for j in range(low, i + 1):
+            dk, dv = 0.0, 0.0
+            to = pl.ds(j * BLK, BLK)
+            for m in range(2):
+                query, cot = heads_in[m]
+                p = score[m, j - low] * inverse[m]
+                ds = (p * (slope[m, j - low] - offset[m])).astype(BF16)
+                dk = dk + jnp.dot(ds, query, preferred_element_type=F32)
+                dv = dv + jnp.dot(p.astype(BF16), cot, preferred_element_type=F32)
+            if i == min(blocks - 1, j + 2):
+                acc[to, 0:HD] = dk
+                acc[to, HD:PAIR] = dv
+            else:
+                acc[to, 0:HD] += dk
+                acc[to, HD:PAIR] += dv
         done = pl.ds(i * BLK, BLK)
         p_ref[done, 0:HD] = (acc[done, 0:HD] * factor).astype(BF16)
         p_ref[done, HD:PAIR] = acc[done, HD:PAIR].astype(BF16)
@@ -299,16 +305,23 @@
         return send.start(piece, piece, at.along_x(way), spare.pop(0) if spare else None)
 
     class Ring:
-        def __init__(self, h):
-            self.h = h
+        def __init__(self, h, sems=None):
+            self.h, self.sems = h, sems
             own = g.at[h, :, rest_rows(x)]
-            self.up = around_copy(own, 1)
-            self.down = around_copy(own, -1)
+            if sems is None:
+                self.up = around_copy(own, 1)
+                self.down = around_copy(own, -1)
+
+        def come(self, name):
+            if self.sems is None:
+                getattr(self, name).wait_recv()
+            else:
+                send.arrived(g.at[self.h, :, rest_rows(x)], self.sems[name])
 
         def pass_on(self):
-            self.up.wait_recv()
+            self.come("up")
             self.up2 = around_copy(g.at[self.h, 0, rest_rows(x + 3)], 1)
-            self.down.wait_recv()
+            self.come("down")
             self.down2 = around_copy(g.at[self.h, 1, rest_rows(x + 1)], -1)
 
         def end(self):
@@ -439,6 +452,8 @@
             around(slot + 2)
 
     cut_ring = {}
+    ring_first = {"up": spare.pop(0), "down": spare.pop(0)}
+    rings[0] = Ring(z, ring_first)
     for hf in (1, 0):
         settle(2 * hf + 1)
         settle(2 * hf)
@@ -448,13 +463,16 @@
         for name, way in ways:
             piece = g.at[z, hf, rest_rows(x)]
             send.start(piece, piece, at.along_z(way), rest_first[name])
+        for name, way in ways:
+            piece = g.at[z, hf, rest_rows(x)]
+            send.start(piece, piece, at.along_x(way), ring_first[name])
     cut_ring["up", 1].wait_recv()
     far_up = around_copy(g.at[z, 1, cut_rows(x + 3)], 1)
     cut_ring["down", 0].wait_recv()
     far_down = around_copy(g.at[z, 0, cut_rows(x + 1)], -1)
-    around(0)
     rest_hop(1)
     around(1)
+    further(0)
     cut_ring["down", 1].wait_recv()
     far_up.wait_recv()
     for name, way in ways:
@@ -463,7 +481,6 @@
     far_down.wait_recv()
     for name, way in ways:
         cut[name, 0] = send_cut(z, 0, way)
-    further(0)
     rest_hop(2)
     further(1)
     for slot in range(8):
@@ -541,8 +558,8 @@
             pltpu.VMEM((TOK, BLK), BF16),
             pltpu.VMEM((BLK, wide), BF16),
             pltpu.VMEM((TOK, PAIR), BF16),
-            pltpu.VMEM((3, BLK, BLK), F32),
-            pltpu.VMEM((3, BLK, BLK), F32),
+            pltpu.VMEM((2, 3, BLK, BLK), F32),
+            pltpu.VMEM((2, 3, BLK, BLK), F32),
             pltpu.VMEM((TOK, PAIR), F32),
             pltpu.VMEM((TOK, PAIR), BF16),
             pltpu.VMEM((4, 3, OWN, PAIR), BF16),

time: 74.5 us -> 73.6 us (0.988)
  Pallas kernels: 73.8 us -> 72.8 us
    pallas_call x1, Pallas kernels: 71 us -> 70 us  [body(): pl.pallas_call(step_kernel, out_shape=results, in_specs=[hbm] * 5 + [pl.B...]
where the time goes in v5:
time: 73.6 us; the launch traced here: 73.5 us
  Pallas kernels  72.8 us (99%)
    pallas_call x1, Pallas kernels, body(): pl.pallas_call(step_kernel, out_shape=results, in_specs=[hbm] * 5 + [pl.B...  70 us
    pallas_call x1, Pallas kernels, body(): pl.pallas_call(write_kernel, out_shape=results, in_specs=[hbm, hbm], out_...  2.83 us

profile of v5, /device:TPU:1, one launch (start us, length us, event | category | flops | bytes accessed | tf_op | source)
XLA Modules:
  0.0 73.5 jit_solution(1114979181187637820)
XLA Ops:
  0.6 70.0 %step.1 = (f32[256,2048]{1,0:T(8,128)}, bf16[256,2048]{1,0:T(8,128)(2,1)}) custom-call(bf16[32,2048]{1,0:T(8,128)(2,1)} %bitcast.10, bf16[1024,256]{1,0:T(8,128)(2,1)} %bitcast.7, bf16[1024,256]{1,0:T(8,128)(2,1)} %bitcast.8, bf16[1024,256]{1,0:T(8,128)(2,1)} %bitcast.9, bf16[256,2048]{1,0:T(8,128)(2,1)} %bitcast.6, s32[1,4]{1,0:T(1,128)} %len_ref.1), custom_call_target="tpu_custom_call" | custom-call | tf_op jit(solution)/shard_map/step/pallas_call | solution.py:549
  70.6 2.8 %write.1 = (f32[256,2048]{1,0:T(8,128)}, bf16[256,2048]{1,0:T(8,128)(2,1)}) custom-call(f32[256,2048]{1,0:T(8,128)} %get-tuple-element.6.fisher_ref, bf16[256,2048]{1,0:T(8,128)(2,1)} %get-tuple-element.7.merged_ref), custom_call_target="tpu_custom_call" | custom-call | tf_op jit(solution)/shard_map/write/pallas_call | solution.py:581

commit v6 on v5

--- a/solution.py
+++ b/solution.py
@@ -173,7 +173,7 @@
 
     def spread_block(z):
         block = kv.at[rows(z, x)]
-        for by in (2, 1, -1):
+        for by in (1, -1, 2):
             spare.append(send.fresh())
             spread.append(send.start(block, block, at.along_x(by), spare[-1]))
 
@@ -211,6 +211,8 @@
             (q_ref[queries, m * HD : m * HD + HD], og_ref[queries, m * HD : m * HD + HD])
             for m in range(2)
         ]
+        both_queries = jnp.concatenate([query for query, cot in heads_in], axis=0)
+        both_cots = jnp.concatenate([cot for query, cot in heads_in], axis=0)
         highest = [jnp.full((1, BLK), NEGATIVE, F32)] * 2
         for j in range(low, i + 1):
             key = kv[pl.ds(j * BLK, BLK), 0:HD]
@@ -236,14 +238,14 @@
         inverse = [1.0 / total[m] for m in range(2)]
         offset = [weighed[m] * inverse[m] for m in range(2)]
         for j in range(low, i + 1):
-            dk, dv = 0.0, 0.0
             to = pl.ds(j * BLK, BLK)
-            for m in range(2):
-                query, cot = heads_in[m]
-                p = score[m, j - low] * inverse[m]
-                ds = (p * (slope[m, j - low] - offset[m])).astype(BF16)
-                dk = dk + jnp.dot(ds, query, preferred_element_type=F32)
-                dv = dv + jnp.dot(p.astype(BF16), cot, preferred_element_type=F32)
+            chances = [score[m, j - low] * inverse[m] for m in range(2)]
+            slopes = [
+                (chances[m] * (slope[m, j - low] - offset[m])).astype(BF16) for m in range(2)
+            ]
+            chances = [p.astype(BF16) for p in chances]
+            dk = jnp.dot(jnp.concatenate(slopes, axis=1), both_queries, preferred_element_type=F32)
+            dv = jnp.dot(jnp.concatenate(chances, axis=1), both_cots, preferred_element_type=F32)
             if i == min(blocks - 1, j + 2):
                 acc[to, 0:HD] = dk
                 acc[to, HD:PAIR] = dv

time: 73.6 us -> 73.7 us (level)
  no operation moved by 1% of the time
where the time goes in v6:
time: 73.7 us; the launch traced here: 73.6 us
  Pallas kernels  73 us (99%)
    pallas_call x1, Pallas kernels, body(): pl.pallas_call(step_kernel, out_shape=results, in_specs=[hbm] * 5 + [pl.B...  70.1 us
    pallas_call x1, Pallas kernels, body(): pl.pallas_call(write_kernel, out_shape=results, in_specs=[hbm, hbm], out_...  2.83 us

profile of v6, /device:TPU:1, one launch (start us, length us, event | category | flops | bytes accessed | tf_op | source)
XLA Modules:
  0.0 73.6 jit_solution(1114465661328323993)
XLA Ops:
  0.6 70.1 %step.1 = (f32[256,2048]{1,0:T(8,128)}, bf16[256,2048]{1,0:T(8,128)(2,1)}) custom-call(bf16[32,2048]{1,0:T(8,128)(2,1)} %bitcast.10, bf16[1024,256]{1,0:T(8,128)(2,1)} %bitcast.7, bf16[1024,256]{1,0:T(8,128)(2,1)} %bitcast.8, bf16[1024,256]{1,0:T(8,128)(2,1)} %bitcast.9, bf16[256,2048]{1,0:T(8,128)(2,1)} %bitcast.6, s32[1,4]{1,0:T(1,128)} %len_ref.1), custom_call_target="tpu_custom_call" | custom-call | tf_op jit(solution)/shard_map/step/pallas_call | solution.py:551
  70.8 2.8 %write.1 = (f32[256,2048]{1,0:T(8,128)}, bf16[256,2048]{1,0:T(8,128)(2,1)}) custom-call(f32[256,2048]{1,0:T(8,128)} %get-tuple-element.6.fisher_ref, bf16[256,2048]{1,0:T(8,128)(2,1)} %get-tuple-element.7.merged_ref), custom_call_target="tpu_custom_call" | custom-call | tf_op jit(solution)/shard_map/write/pallas_call | solution.py:583
